TPU v7x, 32 devices: a whole 2x2x4 slice. The times are simulated.
32 devices in a mesh: fsdp: 8 (over y, x, core), dp: 4 (over z).
Axes of the slice: x: 2, y: 2, z: 4, core: 2. Of those that a mesh axis runs over, the one named last changes fastest.
Arguments:
- incoming_word_states: bfloat16 [512, 64, 768], P(('fsdp', 'dp')), may hold values from -6 to 6
- sentence_number_per_word: int32 [512, 64], P(('fsdp', 'dp')), may hold values from 0 to 3, never falling along the last dimension, each value on 1 to 28 neighbouring positions
- described_picture: int32 [2048], P(('fsdp', 'dp')), may hold values from 0 to 255
- lookup_matrices: bfloat16 [768, 2304], P('fsdp'), may hold values from -0.21875 to 0.21875
- mixer_exit_matrix: bfloat16 [768, 768], P('fsdp'), may hold values from -0.875 to 0.875
- widening_matrix: bfloat16 [768, 3072], P('fsdp'), may hold values from -0.21875 to 0.21875
- narrowing_matrix: bfloat16 [3072, 768], P('fsdp'), may hold values from -0.109375 to 0.109375
- normalizer_multipliers: bfloat16 [2, 768], P(None, 'fsdp'), may hold values from 0.5 to 1.5
- word_offsets: bfloat16 [6, 768], P(None, 'fsdp'), may hold values from -1.25 to 1.25
- widened_offset: bfloat16 [3072], P('fsdp'), may hold values from -1.25 to 1.25
- picture_patches: bfloat16 [256, 50, 768], P(('fsdp', 'dp')), may hold values from -6 to 6
- picture_lookup_matrices: bfloat16 [768, 2304], replicated, may hold values from -0.21875 to 0.21875
- picture_mixer_exit_matrix: bfloat16 [768, 768], replicated, may hold values from -1.5 to 1.5
- picture_widening_matrix: bfloat16 [768, 3072], replicated, may hold values from -0.21875 to 0.21875
- picture_narrowing_matrix: bfloat16 [3072, 768], replicated, may hold values from -0.109375 to 0.109375
- picture_normalizer_multipliers: bfloat16 [2, 768], replicated, may hold values from 0.5 to 1.5
- picture_offsets: bfloat16 [6, 768], replicated, may hold values from -1.25 to 1.25
- picture_widened_offset: bfloat16 [3072], replicated, may hold values from -1.25 to 1.25
- sharpness_coefficient: float32 [1], replicated, may hold values from 0.5 to 2
- objective_offset: float32 [1], replicated, may hold values from -3 to -1
Outputs:
- grad_qkv: float32 [768, 2304], P('fsdp')
- grad_out: float32 [768, 768], P('fsdp')
- grad_up: float32 [768, 3072], P('fsdp')
- grad_down: float32 [3072, 768], P('fsdp')
- grad_gains: float32 [2, 768], P(None, 'fsdp')
- grad_biases: float32 [6, 768], P(None, 'fsdp')
- grad_up_bias: float32 [3072], P('fsdp')
- grad_input: bfloat16 [512, 64, 768], P(('fsdp', 'dp'))
- loss: float32 [2048], P(('fsdp', 'dp'))
Inputs may be any that keep to these rules, and one draw needn't show every extreme that they name: `sentence_number_per_word`: in each text row the segment ids number its 4 captions in order, never falling; every caption has at least one token. described_picture(r * 4 + c) is the image of the caption with segment id c in text row r.
All inputs are finite; a program needn't handle non-finite values.
Results may differ from a plain program's by a relative error of at most 0.011.
Values may be sent and summed in bfloat16 or wider, within the bound.
A program may use at most 192 MiB of HBM per device.

v0:
```python
import math

import jax
import jax.numpy as jnp
from jax import lax
from jax.sharding import PartitionSpec as P

HEAD_DIM = 64
CAPS = 4


def layer_norm(values, gain, shift):
    centred = values - jnp.mean(values, axis=-1, keepdims=True)
    inverse = lax.rsqrt(jnp.mean(centred * centred, axis=-1, keepdims=True) + 1e-06)
    scaled = centred * inverse
    return (scaled * gain + shift, scaled, inverse)


def norm_back(grad_scaled, scaled, inverse):
    first_mean = jnp.mean(grad_scaled, axis=-1, keepdims=True)
    second_mean = jnp.mean(grad_scaled * scaled, axis=-1, keepdims=True)
    return inverse * (grad_scaled - first_mean - scaled * second_mean)


def gelu_exact(values):
    return jax.nn.gelu(values, approximate=False)


def forward_block(flat, rows, length, mask, weights):
    qkv_w, out_w, up_w, down_w, gains_low, biases_low, up_b = weights
    gains = gains_low.astype(jnp.float32)
    biases = biases_low.astype(jnp.float32)
    channel_count = flat.shape[-1]
    heads = channel_count // HEAD_DIM
    scale = 1.0 / math.sqrt(HEAD_DIM)
    first, scaled_one, inverse_one = layer_norm(flat, gains[0], biases[4])
    first_low = first.astype(jnp.bfloat16)
    mixed = jnp.dot(first_low, qkv_w, preferred_element_type=jnp.float32)
    query = (
        ((mixed[:, :channel_count] + biases[0]) * scale)
        .astype(jnp.bfloat16)
        .reshape(rows, length, heads, HEAD_DIM)
    )
    key_low = (
        mixed[:, channel_count : 2 * channel_count]
        .astype(jnp.bfloat16)
        .reshape(rows, length, heads, HEAD_DIM)
    )
    value_low = (
        (mixed[:, 2 * channel_count :] + biases[1])
        .astype(jnp.bfloat16)
        .reshape(rows, length, heads, HEAD_DIM)
    )
    scores = jnp.einsum("rqhd,rkhd->rhqk", query, key_low, preferred_element_type=jnp.float32)
    if mask is not None:
        scores = jnp.where(mask[:, None], scores, -1e30)
    probs = jax.nn.softmax(scores, axis=-1)
    probs_low = probs.astype(jnp.bfloat16)
    attended = jnp.einsum(
        "rhqk,rkhd->rqhd", probs_low, value_low, preferred_element_type=jnp.float32
    )
    attended = attended.astype(jnp.bfloat16).reshape(rows * length, channel_count)
    middle = flat + (jnp.dot(attended, out_w, preferred_element_type=jnp.float32) + biases[2])
    second, scaled_two, inverse_two = layer_norm(middle, gains[1], biases[5])
    second_low = second.astype(jnp.bfloat16)
    hidden = jnp.dot(second_low, up_w, preferred_element_type=jnp.float32) + up_b.astype(
        jnp.float32
    )
    active = gelu_exact(hidden).astype(jnp.bfloat16)
    output = middle + (jnp.dot(active, down_w, preferred_element_type=jnp.float32) + biases[3])
    saved = (
        scaled_one,
        inverse_one,
        first_low,
        query,
        key_low,
        value_low,
        probs,
        probs_low,
        attended,
        scaled_two,
        inverse_two,
        second_low,
        hidden,
        active,
    )
    return (output, saved)


def backward_block(grad_output, saved, weights, rows, length):
    qkv_w, out_w, up_w, down_w, gains_low, biases_low, up_b = weights
    gains = gains_low.astype(jnp.float32)
    (
        scaled_one,
        inverse_one,
        first_low,
        query,
        key_low,
        value_low,
        probs,
        probs_low,
        attended,
        scaled_two,
        inverse_two,
        second_low,
        hidden,
        active,
    ) = saved
    channel_count = grad_output.shape[-1]
    heads = channel_count // HEAD_DIM
    scale = 1.0 / math.sqrt(HEAD_DIM)
    count = rows * length
    down_grad = grad_output.astype(jnp.bfloat16)
    grad_down_bias = jnp.sum(down_grad, axis=0, dtype=jnp.float32)
    grad_down_w = jnp.einsum("nf,nd->fd", active, down_grad, preferred_element_type=jnp.float32)
    active_grad = jnp.einsum("nd,fd->nf", down_grad, down_w, preferred_element_type=jnp.float32)
    gelu_back = jax.vjp(gelu_exact, hidden)[1]
    hidden_grad = gelu_back(active_grad)[0].astype(jnp.bfloat16)
    grad_up_bias = jnp.sum(hidden_grad, axis=0, dtype=jnp.float32)
    grad_up_w = jnp.einsum("nd,nf->df", second_low, hidden_grad, preferred_element_type=jnp.float32)
    second_grad = jnp.einsum("nf,df->nd", hidden_grad, up_w, preferred_element_type=jnp.float32)
    grad_gain_two = jnp.sum(second_grad * scaled_two, axis=0)
    grad_shift_two = jnp.sum(second_grad, axis=0)
    middle_grad = grad_output + norm_back(second_grad * gains[1], scaled_two, inverse_two)
    branch_grad = middle_grad.astype(jnp.bfloat16)
    grad_out_bias = jnp.sum(branch_grad, axis=0, dtype=jnp.float32)
    grad_out_w = jnp.einsum("nd,ne->de", attended, branch_grad, preferred_element_type=jnp.float32)
    attended_grad = jnp.einsum("ne,de->nd", branch_grad, out_w, preferred_element_type=jnp.float32)
    attended_grad = attended_grad.astype(jnp.bfloat16).reshape(rows, length, heads, HEAD_DIM)
    probs_grad = jnp.einsum(
        "rqhd,rkhd->rhqk", attended_grad, value_low, preferred_element_type=jnp.float32
    )
    value_grad = jnp.einsum(
        "rhqk,rqhd->rkhd", probs_low, attended_grad, preferred_element_type=jnp.float32
    ).astype(jnp.bfloat16)
    score_grad = probs * (probs_grad - jnp.sum(probs * probs_grad, axis=-1, keepdims=True))
    score_grad = score_grad.astype(jnp.bfloat16)
    query_grad = jnp.einsum(
        "rhqk,rkhd->rqhd", score_grad, key_low, preferred_element_type=jnp.float32
    ).astype(jnp.bfloat16)
    key_grad = jnp.einsum(
        "rhqk,rqhd->rkhd", score_grad, query, preferred_element_type=jnp.float32
    ).astype(jnp.bfloat16)
    query_flat = query_grad.reshape(count, channel_count) * scale
    value_flat = value_grad.reshape(count, channel_count)
    mixed_grad = jnp.concatenate(
        [query_flat, key_grad.reshape(count, channel_count), value_flat], axis=1
    )
    grad_query_bias = jnp.sum(query_flat, axis=0, dtype=jnp.float32)
    grad_value_bias = jnp.sum(value_flat, axis=0, dtype=jnp.float32)
    grad_qkv_w = jnp.einsum("nd,ne->de", first_low, mixed_grad, preferred_element_type=jnp.float32)
    first_grad = jnp.einsum("ne,de->nd", mixed_grad, qkv_w, preferred_element_type=jnp.float32)
    grad_gain_one = jnp.sum(first_grad * scaled_one, axis=0)
    grad_shift_one = jnp.sum(first_grad, axis=0)
    input_grad = middle_grad + norm_back(first_grad * gains[0], scaled_one, inverse_one)
    grad_gains = jnp.stack([grad_gain_one, grad_gain_two])
    grad_biases = jnp.stack(
        [
            grad_query_bias,
            grad_value_bias,
            grad_out_bias,
            grad_down_bias,
            grad_shift_one,
            grad_shift_two,
        ]
    )
    return (
        input_grad,
        (grad_qkv_w, grad_out_w, grad_up_w, grad_down_w, grad_gains, grad_biases, grad_up_bias),
    )


def per_device(
    incoming_word_states,
    sentence_number_per_word,
    described_picture,
    lookup_matrices,
    mixer_exit_matrix,
    widening_matrix,
    narrowing_matrix,
    normalizer_multipliers,
    word_offsets,
    widened_offset,
    picture_patches,
    picture_lookup_matrices,
    picture_mixer_exit_matrix,
    picture_widening_matrix,
    picture_narrowing_matrix,
    picture_normalizer_multipliers,
    picture_offsets,
    picture_widened_offset,
    sharpness_coefficient,
    objective_offset,
):
    rows, length, channel_count = incoming_word_states.shape
    whole = (
        lax.all_gather(lookup_matrices, "fsdp", axis=0, tiled=True),
        lax.all_gather(mixer_exit_matrix, "fsdp", axis=0, tiled=True),
        lax.all_gather(widening_matrix, "fsdp", axis=0, tiled=True),
        lax.all_gather(narrowing_matrix, "fsdp", axis=0, tiled=True),
        lax.all_gather(normalizer_multipliers, "fsdp", axis=1, tiled=True),
        lax.all_gather(word_offsets, "fsdp", axis=1, tiled=True),
        lax.all_gather(widened_offset, "fsdp", axis=0, tiled=True),
    )
    image_rows, image_length = (picture_patches.shape[0], picture_patches.shape[1])
    image_flat = picture_patches.astype(jnp.float32).reshape(
        image_rows * image_length, channel_count
    )
    image_weights = (
        picture_lookup_matrices,
        picture_mixer_exit_matrix,
        picture_widening_matrix,
        picture_narrowing_matrix,
        picture_normalizer_multipliers,
        picture_offsets,
        picture_widened_offset,
    )
    image_result = forward_block(image_flat, image_rows, image_length, None, image_weights)[0]
    image_token = image_result.reshape(image_rows, image_length, channel_count)[:, 0, :]
    image_embed = (
        image_token * lax.rsqrt(jnp.mean(image_token * image_token, axis=-1, keepdims=True) + 1e-06)
    ).astype(jnp.bfloat16)
    mask = sentence_number_per_word[:, :, None] == sentence_number_per_word[:, None, :]
    flat = incoming_word_states.astype(jnp.float32).reshape(rows * length, channel_count)
    text_result = forward_block(flat, rows, length, mask, whole)[0]
    member = (sentence_number_per_word[:, :, None] == jnp.arange(CAPS, dtype=jnp.int32)).astype(
        jnp.float32
    )
    counts = jnp.sum(member, axis=1)[:, :, None]
    pooled = (
        jnp.einsum(
            "rsc,rsd->rcd",
            member,
            text_result.reshape(rows, length, channel_count),
            precision=lax.Precision.HIGHEST,
        )
        / counts
    )
    pooled = pooled.reshape(rows * CAPS, channel_count)
    inverse = lax.rsqrt(jnp.mean(pooled * pooled, axis=-1, keepdims=True) + 1e-06)
    embed = pooled * inverse
    embed_low = embed.astype(jnp.bfloat16)
    multiplier_amount = sharpness_coefficient[0] / math.sqrt(channel_count)
    piece = lax.all_gather(image_embed, ("fsdp", "dp"), axis=0, tiled=True)
    unscaled_similarity = jnp.einsum(
        "cd,nd->cn", embed_low, piece, preferred_element_type=jnp.float32
    )
    match_similarity = multiplier_amount * unscaled_similarity + objective_offset[0]
    positive = described_picture[:, None] == jnp.arange(piece.shape[0], dtype=jnp.int32)[None, :]
    labels = jnp.where(positive, 1.0, -1.0)
    total = jnp.sum(jax.nn.softplus(-labels * match_similarity), axis=1)
    slope = (
        (jax.nn.sigmoid(match_similarity) - positive.astype(jnp.float32)) * multiplier_amount
    ).astype(jnp.bfloat16)
    grad_embed = jnp.einsum("cn,nd->cd", slope, piece, preferred_element_type=jnp.float32)
    images_all = image_rows * lax.axis_size("fsdp") * lax.axis_size("dp")
    loss = total / images_all
    pooled_grad = inverse * (
        grad_embed - embed * jnp.mean(grad_embed * embed, axis=-1, keepdims=True)
    )
    per_caption = pooled_grad.reshape(rows, CAPS, channel_count) / counts
    token_grad = jnp.einsum(
        "rsc,rcd->rsd", member, per_caption, precision=lax.Precision.HIGHEST
    ).reshape(rows * length, channel_count)
    again = (
        lax.all_gather(lookup_matrices, "fsdp", axis=0, tiled=True),
        lax.all_gather(mixer_exit_matrix, "fsdp", axis=0, tiled=True),
        lax.all_gather(widening_matrix, "fsdp", axis=0, tiled=True),
        lax.all_gather(narrowing_matrix, "fsdp", axis=0, tiled=True),
        lax.all_gather(normalizer_multipliers, "fsdp", axis=1, tiled=True),
        lax.all_gather(word_offsets, "fsdp", axis=1, tiled=True),
        lax.all_gather(widened_offset, "fsdp", axis=0, tiled=True),
    )
    saved = forward_block(flat, rows, length, mask, again)[1]
    input_grad, grads = backward_block(token_grad, saved, again, rows, length)
    owned = (
        lax.psum_scatter(grads[0], "fsdp", scatter_dimension=0, tiled=True),
        lax.psum_scatter(grads[1], "fsdp", scatter_dimension=0, tiled=True),
        lax.psum_scatter(grads[2], "fsdp", scatter_dimension=0, tiled=True),
        lax.psum_scatter(grads[3], "fsdp", scatter_dimension=0, tiled=True),
        lax.psum_scatter(grads[4], "fsdp", scatter_dimension=1, tiled=True),
        lax.psum_scatter(grads[5], "fsdp", scatter_dimension=1, tiled=True),
        lax.psum_scatter(grads[6], "fsdp", scatter_dimension=0, tiled=True),
    )
    summed = (
        lax.psum(owned[0].astype(jnp.bfloat16), "dp").astype(jnp.float32),
        lax.psum(owned[1].astype(jnp.bfloat16), "dp").astype(jnp.float32),
        lax.psum(owned[2].astype(jnp.bfloat16), "dp").astype(jnp.float32),
        lax.psum(owned[3].astype(jnp.bfloat16), "dp").astype(jnp.float32),
        lax.psum(owned[4].astype(jnp.bfloat16), "dp").astype(jnp.float32),
        lax.psum(owned[5].astype(jnp.bfloat16), "dp").astype(jnp.float32),
        lax.psum(owned[6].astype(jnp.bfloat16), "dp").astype(jnp.float32),
    )
    grad_input = input_grad.astype(jnp.bfloat16).reshape(rows, length, channel_count)
    return (
        summed[0],
        summed[1],
        summed[2],
        summed[3],
        summed[4],
        summed[5],
        summed[6],
        grad_input,
        loss,
    )


def solution(mesh):
    return jax.shard_map(
        per_device,
        mesh=mesh,
        in_specs=(
            P(("fsdp", "dp"), None, None),
            P(("fsdp", "dp"), None),
            P(("fsdp", "dp")),
            P("fsdp", None),
            P("fsdp", None),
            P("fsdp", None),
            P("fsdp", None),
            P(None, "fsdp"),
            P(None, "fsdp"),
            P("fsdp"),
            P(("fsdp", "dp"), None, None),
            P(),
            P(),
            P(),
            P(),
            P(),
            P(),
            P(),
            P(),
            P(),
        ),
        out_specs=(
            P("fsdp", None),
            P("fsdp", None),
            P("fsdp", None),
            P("fsdp", None),
            P(None, "fsdp"),
            P(None, "fsdp"),
            P("fsdp"),
            P(("fsdp", "dp"), None, None),
            P(("fsdp", "dp")),
        ),
        check_vma=False,
    )
```

profile of v0, /device:TPU:0, one launch (start us, length us, event | category | flops | bytes accessed | tf_op | source)
XLA Modules:
  0.0 798.2 jit_solution(830218209137158584)
XLA Ops:
  25.4 3.0 fusion.65
  32.4 4.3 fusion.57
  36.8 3.2 fusion.136
  44.4 5.4 fusion.52
  53.3 2.6 fusion.141
  56.3 18.7 %fusion.55 = f32[400,768]{1,0:T(8,128)} fusion(f32[400,768]{1,0:T(8,128)S(1)} %get-tuple-element.56, bf16[3072,768]{1,0:T(8,128)(2,1)} %param.34, bf16[768,3072]{1,0:T(8,128)(2,1)} %param.33, f32[3072]{0:T(1024)S(1)} %convert_element_type.223, f32[768]{0:T(1024)S(1)} %copy-done.40, f32[768]{0:T(1024)S(1)} %copy-done.39, f32[768]{0:T(1024)S(1)} %copy-done.41, ...), kind=kOutput, calls=%fused_computation.109 | convolution fusion | flops 3858124800 | bytes 11919488 | tf_op jit(solution)/shard_map/dot_general | solution.py:70
  76.7 73.5 %all_gather.38 = bf16[256,768]{1,0:T(8,128)(2,1)S(1)} all-gather(bf16[8,768]{1,0:T(8,128)(2,1)S(1)} %fusion.88), channel_id=1, replica_groups=mesh['fsdp'=8,'dp'=4] {'fsdp','dp'}, dimensions={0}, use_global_device_ids=true | all-gather | bytes 405504 | tf_op jit(solution)/shard_map/all_gather | solution.py:244
  150.2 7.9 all-gather.1
  159.0 8.8 %all-gather = bf16[8,96,2]{1,2,0:T(2,128)(2,1)S(1)} all-gather(bf16[1,96,2]{1,2,0:T(2,128)(2,1)S(1)} %bitcast.133), channel_id=1, replica_groups=mesh['fsdp'=8,'dp'=4] {'fsdp'}, dimensions={0}, use_global_device_ids=true | all-gather | bytes 3456 | tf_op jit(solution)/shard_map/all_gather | solution.py:270
  167.9 7.9 all-gather.2
  179.1 6.4 fusion.142
  188.7 4.0 reshape.284
  192.7 6.4 copy.127
  199.1 6.1 reshape.266
  205.3 5.9 reshape.285
  211.2 3.2 fusion.46
  221.7 3.2 reshape.237
  224.9 3.8 fusion.135
  229.3 36.2 %multiply_convert_fusion = (bf16[1024,3072]{1,0:T(8,128)(2,1)}, f32[1024,3072]{1,0:T(8,128)}, f32[1024,3072]{1,0:T(8,128)}) fusion(f32[3072]{0:T(1024)} %bitcast.130, bf16[768,3072]{1,0:T(8,128)(2,1)} %all-gather.12.cloned.1.call-done, f32[1024,768]{1,0:T(8,128)S(1)} %get-tuple-element.53, f32[768]{0:T(1024)S(1)} %get-tuple-element.18, ...), kind=kOutput, calls=%fused_computation.6 | convolution fusion | flops 5043388416 | bytes 39348224 | tf_op jit(solution)/shard_map/dot_general | solution.py:66
  265.5 8.6 %add_add_fusion = f32[1024,768]{1,0:T(8,128)S(1)} fusion(f32[1024,768]{1,0:T(8,128)S(1)} %get-tuple-element.53, bf16[1024,3072]{1,0:T(8,128)(2,1)} %get-tuple-element.42, bf16[3072,768]{1,0:T(8,128)(2,1)} %all-gather.14.cloned.1.call-done, f32[768]{0:T(1024)} %get-tuple-element.17), kind=kOutput, calls=%fused_computation.80 | convolution fusion | flops 4833411072 | bytes 17304576 | tf_op jit(solution)/shard_map/dot_general | solution.py:70
  288.9 18.8 %convert_reduce_fusion = (f32[3072]{0:T(1024)S(1)}, bf16[1024,3072]{1,0:T(8,128)(2,1)}) fusion(f32[1024,3072]{1,0:T(8,128)} %get-tuple-element.43, bf16[1024,768]{1,0:T(8,128)(2,1)} %get-tuple-element.49, bf16[3072,768]{1,0:T(8,128)(2,1)} %all-gather.14.cloned.1.call-done, f32[1024,3072]{1,0:T(8,128)} %get-tuple-element.54, f32[3072]{0:T(1024)S(1)} %bitcast.131), kind=kOutput, calls=%fused_computation.4 | convolution fusion | flops 4885312512 | bytes 37773312 | tf_op jit(solution)/shard_map/nd,fd->nf/dot_general | solution.py:116
  307.7 9.2 %multiply_reduce_fusion.1 = (f32[768]{0:T(1024)S(1)}, f32[1024]{0:T(1024)S(1)}, f32[1024]{0:T(1024)S(1)}, f32[768]{0:T(1024)S(1)}, f32[1024,768]{1,0:T(8,128)S(1)}) fusion(f32[1024,768]{1,0:T(8,128)S(1)} %get-tuple-element.53, f32[1024]{0:T(1024)S(1)} %add_rsqrt_fusion.3, f32[1024]{0:T(1024)S(1)} %broadcast_multiply_fusion.6, f32[768]{0:T(1024)S(1)} %copy-done.25, ...), kind=kOutput, calls=%fused_computation.75 | convolution fusion | flops 4838912000 | bytes 17327104 | tf_op jit(solution)/shard_map/nf,df->nd/dot_general | solution.py:121
  320.1 2.9 fusion.96
  322.9 4.8 convolution_convert_fusion
  327.8 5.9 reshape.267
  333.7 9.8 %multiply_reduce_fusion = (f32[16,12,64]{2,1,0:T(8,128)S(1)}, f32[16,12,64,64]{2,3,1,0:T(8,128)}) fusion(f32[16,12,64,64]{2,3,1,0:T(8,128)} %copy-done.10, f32[16,12,64]{2,1,0:T(8,128)S(1)} %copy-done.22, bf16[16,64,12,64]{3,2,1,0:T(8,128)(2,1)} %reshape.285, bf16[16,64,12,64]{3,2,1,0:T(8,128)(2,1)} %reshape.267), kind=kOutput, calls=%fused_computation.24 | convolution fusion | flops 103010304 | bytes 9535488 | tf_op jit(solution)/shard_map/rqhd,rkhd->rhqk/dot_general | solution.py:130
  343.8 7.4 convert_reduce_fusion.1
  351.2 5.3 copy.131
  356.5 5.4 reshape.250
  361.9 6.8 multiply_convert_fusion.1
  370.5 4.2 copy.129
  374.7 5.4 reshape.249
  380.2 6.8 convert_reduce_fusion.2
  387.0 5.3 copy.126
  392.2 5.6 mul.354
  402.5 6.0 fusion.143
  408.5 10.1 %fusion.144 = f32[3072,768]{1,0:T(8,128)} fusion(bf16[1024,3072]{1,0:T(8,128)(2,1)} %get-tuple-element.42, bf16[1024,768]{1,0:T(8,128)(2,1)} %get-tuple-element.49), kind=kOutput, calls=%fused_computation.246 | convolution fusion | flops 4831838208 | bytes 17301504 | tf_op jit(solution)/shard_map/nf,nd->fd/dot_general | solution.py:115
  419.4 11.0 %fusion.131 = f32[768,3072]{1,0:T(8,128)} fusion(bf16[1024,3072]{1,0:T(8,128)(2,1)} %get-tuple-element.70, f32[1024,768]{1,0:T(8,128)S(1)} %get-tuple-element.53, f32[768]{0:T(1024)S(1)} %copy-done.28, f32[768]{0:T(1024)S(1)} %copy-done.25, f32[1024]{0:T(1024)S(1)} %add_rsqrt_fusion.3, f32[1024]{0:T(1024)S(1)} %broadcast_multiply_fusion.6), kind=kOutput, calls=%fused_computation.238 | convolution fusion | flops 4835770368 | bytes 18888704 | tf_op jit(solution)/shard_map/nd,nf->df/dot_general | solution.py:120
  432.3 9.6 %fusion.34 = (f32[1024]{0:T(1024)S(1)}, f32[768]{0:T(1024)S(1)}, f32[1024]{0:T(1024)S(1)}, f32[768]{0:T(1024)S(1)}, f32[1024,768]{1,0:T(8,128)}) fusion(bf16[16,64,768]{2,1,0:T(8,128)(2,1)S(1)} %copy-done.5, f32[768]{0:T(1024)S(1)} %copy-done.34, f32[1024]{0:T(1024)S(1)} %copy-done.32, f32[1024]{0:T(1024)S(1)} %copy-done.30, ...), kind=kOutput, calls=%fused_computation.68 | convolution fusion | flops 3631739392 | bytes 13001728 | tf_op jit(solution)/shard_map/ne,de->nd/dot_general | solution.py:152
  445.9 25.8 %reduce-scatter.11.cloned.1.call-done = f32[96,2304]{1,0:T(8,128)} async-done(((f32[768,2304]{1,0:T(8,128)}), f32[96,2304]{1,0:T(8,128)}) %reduce-scatter.11.cloned.1.call-update) | async-done | bytes 884752 | tf_op jit(solution)/shard_map/reduce_scatter | solution.py:277
  473.7 78.4 %reduce-scatter.17.cloned.1.call-done = f32[384,768]{1,0:T(8,128)} async-done(((f32[3072,768]{1,0:T(8,128)}), f32[384,768]{1,0:T(8,128)}) %reduce-scatter.17.cloned.1.call-update) | async-done | bytes 1179664 | tf_op jit(solution)/shard_map/reduce_scatter | solution.py:280
  554.2 78.2 %reduce-scatter.15.cloned.1.call-done = f32[96,3072]{1,0:T(8,128)} async-done(((f32[768,3072]{1,0:T(8,128)}), f32[96,3072]{1,0:T(8,128)}) %reduce-scatter.15.cloned.1.call-update) | async-done | bytes 1179664 | tf_op jit(solution)/shard_map/reduce_scatter | solution.py:279
  635.8 22.9 %all-reduce = bf16[3072]{0:T(1024)(128)(2,1)S(1)} all-reduce(f32[3072]{0:T(1024)S(1)} %get-tuple-element.69), channel_id=8, replica_groups=mesh['fsdp'=8,'dp'=4] {'fsdp'}, use_global_device_ids=true, to_apply=%region_40.41.clone | all-reduce | flops 3072 | bytes 18432
  659.3 4.9 fusion.38
  664.3 5.2 reduce-scatter.19.cloned.1.call-done
  670.3 36.0 %reduce-scatter.21.cloned.1.call-done = f32[96,6]{1,0:T(8,128)} async-done(((f32[768,6]{1,0:T(8,128)}), f32[96,6]{1,0:T(8,128)}) %reduce-scatter.21.cloned.1.call-update) | async-done | bytes 2320
  707.2 12.5 %all-reduce.1 = (bf16[2,96]{1,0:T(2,128)(2,1)}, bf16[6,96]{1,0:T(8,128)(2,1)S(1)}, bf16[384]{0:T(512)(128)(2,1)}) all-reduce(bf16[2,96]{1,0:T(2,128)(2,1)S(1)} %copy.137, bf16[6,96]{1,0:T(8,128)(2,1)S(1)} %copy.139, bf16[384]{0:T(512)(128)(2,1)S(1)} %dynamic-slice.3), channel_id=1, replica_groups=mesh['fsdp'=8,'dp'=4] {'dp'}, use_global_device_ids=true, to_apply=%region_30.31 | all-reduce | flops 1152 | bytes 4608 | tf_op jit(solution)/shard_map/psum | solution.py:290
  722.7 62.4 %all-reduce.5.cloned.1.call-done = (bf16[96,2304]{1,0:T(8,128)(2,1)}, bf16[96,768]{1,0:T(8,128)(2,1)}, bf16[96,3072]{1,0:T(8,128)(2,1)}, bf16[384,768]{1,0:T(8,128)(2,1)}) async-done(((bf16[96,2304]{1,0:T(8,128)(2,1)}, bf16[96,768]{1,0:T(8,128)(2,1)}, bf16[96,3072]{1,0:T(8,128)(2,1)}, bf16[384,768]{1,0:T(8,128)(2,1)}), (bf16[96,2304]{1,0:T(8,128)(2,1)}, bf16[96,768]{1,0:T(8,128)(2,1)}, ...) | async-done | bytes 1769488 | tf_op jit(solution)/shard_map/psum | solution.py:286
  (228 shorter events, 95.2 us)
Async XLA Ops:
  7.2 18.2 %copy-start = (bf16[768,2304]{1,0:T(8,128)(2,1)S(1)}, bf16[768,2304]{1,0:T(8,128)(2,1)}, u32[]{:S(2)}) copy-start(bf16[768,2304]{1,0:T(8,128)(2,1)} %param.31) | copy-start | bytes 10616836
  7.2 10.5 %copy-start.43 = (bf16[2,768]{1,0:T(2,128)(2,1)S(1)}, bf16[2,768]{1,0:T(2,128)(2,1)}, u32[]{:S(2)}) copy-start(bf16[2,768]{1,0:T(2,128)(2,1)} %param.35) | copy-start | bytes 9220
  7.2 171.9 %all-gather.8.cloned.1.call-start = ((), (), s32[]{:S(2)}) async-start(), calls=%async_computation.6 | async-start | bytes 3981312 | tf_op jit(solution)/shard_map/all_gather | solution.py:266
  7.9 217.0 %all-gather.10.cloned.1.call-start = ((), (), s32[]{:S(2)}) async-start(), calls=%async_computation.7 | async-start | bytes 1327104 | tf_op jit(solution)/shard_map/all_gather | solution.py:198
  8.7 220.6 %all-gather.12.cloned.1.call-start = ((), (), s32[]{:S(2)}) async-start(), calls=%async_computation.8 | async-start | bytes 5308416 | tf_op jit(solution)/shard_map/all_gather | solution.py:199
  9.4 256.1 %all-gather.14.cloned.1.call-start = ((), (), s32[]{:S(2)}) async-start(), calls=%async_computation.9 | async-start | bytes 5308416 | tf_op jit(solution)/shard_map/all_gather | solution.py:200
  10.0 434.2 %reduce-scatter.13.cloned.1.call-start = ((), (), s32[]{:S(2)}) async-start(), calls=%async_computation.11 | async-start | bytes 2654208 | tf_op jit(solution)/shard_map/reduce_scatter | solution.py:278
  36.8 3.2 copy-start.4
  40.0 2.5 copy-start.12
  40.9 136.8 %copy-start.29 = (f32[1024]{0:T(1024)}, f32[1024]{0:T(1024)S(1)}, u32[]{:S(2)}) copy-start(f32[1024]{0:T(1024)S(1)} %div.102) | copy-start | bytes 12292
  53.3 3.0 copy-start.38
  53.3 3.0 copy-start.39
  53.3 3.0 copy-start.40
  53.3 3.0 copy-start.41
  56.3 93.9 %copy-start.44 = (bf16[6,96]{1,0:T(8,128)(2,1)S(1)}, bf16[6,96]{1,0:T(8,128)(2,1)}, u32[]{:S(2)}) copy-start(bf16[6,96]{1,0:T(8,128)(2,1)} %param.28) | copy-start | bytes 3460
  75.0 83.9 %copy-start.46 = (bf16[2,96]{1,0:T(2,128)(2,1)S(1)}, bf16[2,96]{1,0:T(2,128)(2,1)}, u32[]{:S(2)}) copy-start(bf16[2,96]{1,0:T(2,128)(2,1)} %param.27) | copy-start | bytes 1156
  75.0 92.8 %copy-start.45 = (bf16[384]{0:T(512)(128)(2,1)S(1)}, bf16[384]{0:T(512)(128)(2,1)}, u32[]{:S(2)}) copy-start(bf16[384]{0:T(512)(128)(2,1)} %param.29) | copy-start | bytes 2308
  158.9 70.4 %copy-start.27 = (f32[768]{0:T(1024)}, f32[768]{0:T(1024)S(1)}, u32[]{:S(2)}) copy-start(f32[768]{0:T(1024)S(1)} %get-tuple-element.18) | copy-start | bytes 9220
  158.9 26.6 %copy-start.31 = (f32[1024]{0:T(1024)}, f32[1024]{0:T(1024)S(1)}, u32[]{:S(2)}) copy-start(f32[1024]{0:T(1024)S(1)} %rsqrt.60) | copy-start | bytes 12292
  167.9 9.9 %copy-start.33 = (f32[768]{0:T(1024)}, f32[768]{0:T(1024)S(1)}, u32[]{:S(2)}) copy-start(f32[768]{0:T(1024)S(1)} %get-tuple-element.30) | copy-start | bytes 9220
  167.9 61.5 %copy-start.24 = (f32[768]{0:T(1024)}, f32[768]{0:T(1024)S(1)}, u32[]{:S(2)}) copy-start(f32[768]{0:T(1024)S(1)} %get-tuple-element.29) | copy-start | bytes 9220
  179.1 6.4 copy-start.13
  199.1 12.0 %copy-start.2 = (bf16[16,64,12,64]{1,3,2,0:T(8,128)(2,1)}, bf16[16,64,12,64]{1,3,2,0:T(8,128)(2,1)S(1)}, u32[]{:S(2)}) copy-start(bf16[16,64,12,64]{1,3,2,0:T(8,128)(2,1)S(1)} %copy.127) | copy-start | bytes 4718596
  211.2 3.2 copy-start.23
  214.4 2.9 copy-start.11
  216.6 2.6 copy-start.10
  221.7 3.2 copy-start.42
  265.5 8.6 %copy-start.19 = (s32[16,64]{1,0:T(8,128)S(1)}, s32[16,64]{1,0:T(8,128)}, u32[]{:S(2)}) copy-start(s32[16,64]{1,0:T(8,128)} %param.21) | copy-start | bytes 12292
  265.5 8.6 %copy-start.26 = (f32[16,4]{1,0:T(8,128)S(1)}, f32[16,4]{1,0:T(8,128)}, u32[]{:S(2)}) copy-start(f32[16,4]{1,0:T(8,128)} %convert_reduce_fusion.7) | copy-start | bytes 772
  288.9 18.8 %copy-start.25 = (f32[768]{0:T(1024)S(1)}, f32[768]{0:T(1024)}, u32[]{:S(2)}) copy-start(f32[768]{0:T(1024)} %copy-done.24) | copy-start | bytes 9220
  316.9 3.1 copy-start.15
  327.8 5.9 copy-start.22
  343.6 128.2 %reduce-scatter.11.cloned.1.call-start = ((), (), s32[]{:S(2)}) async-start(), calls=%async_computation.10 | async-start | bytes 7962624 | tf_op jit(solution)/shard_map/reduce_scatter | solution.py:277
  361.9 6.8 copy-start.3
  397.8 2.3 copy-start.8
  399.7 2.8 copy-start.14
  400.3 2.2 copy-start.16
  408.5 143.6 %reduce-scatter.17.cloned.1.call-start = ((), (), s32[]{:S(2)}) async-start(), calls=%async_computation.13 | async-start | bytes 10616832 | tf_op jit(solution)/shard_map/reduce_scatter | solution.py:280
  418.7 213.7 %reduce-scatter.15.cloned.1.call-start = ((), (), s32[]{:S(2)}) async-start(), calls=%async_computation.12 | async-start | bytes 10616832 | tf_op jit(solution)/shard_map/reduce_scatter | solution.py:279
  430.4 1.9 copy-start.34
  430.4 239.0 %reduce-scatter.19.cloned.1.call-start = ((), (), s32[]{:S(2)}) async-start(), calls=%async_computation.14 | async-start | bytes 442368
  442.9 263.4 %reduce-scatter.21.cloned.1.call-start = ((), (), s32[]{:S(2)}) async-start(), calls=%async_computation.15 | async-start | bytes 442368
  444.2 340.9 %all-reduce.5.cloned.1.call-start = ((), (), s32[]{:S(2)}) async-start(), calls=%async_computation.16 | async-start | bytes 3538944 | tf_op jit(solution)/shard_map/psum | solution.py:286
  445.9 188.7 %copy-start.48 = (u32[32]{0:T(128)S(1)}, u32[32]{0:T(128)}, u32[]{:S(2)}) copy-start(u32[32]{0:T(128)} %constant.24) | copy-start | bytes 388
  445.9 212.9 %copy-start.47 = (f32[64]{0:T(128)S(1)}, f32[64]{0:T(128)}, u32[]{:S(2)}) copy-start(f32[64]{0:T(128)} %get-tuple-element.71) | copy-start | bytes 772
  659.3 131.9 %copy-start.1 = (bf16[768,2304]{1,0:T(8,128)(2,1)S(1)}, bf16[768,2304]{1,0:T(8,128)(2,1)}, u32[]{:S(2)}) copy-start(bf16[768,2304]{1,0:T(8,128)(2,1)} %param.31) | copy-start | bytes 10616836
  785.1 4.4 copy-start.17
  785.1 5.4 copy-start.20
  (12 other events, 17.4 us)
Sparse Core Ops, SparseCore 0:
  9.9 36.5 all-gather.7
  48.4 23.9 all-gather.9
  74.2 39.5 all-gather.11
  115.6 39.2 all-gather.13
  343.7 39.5 reduce-scatter.12
  408.6 63.0 reduce-scatter.10
  475.2 76.8 reduce-scatter.16
  555.6 76.8 reduce-scatter.14
  635.5 33.9 reduce-scatter.18
  672.4 33.8 reduce-scatter.20
  709.5 75.5 all-reduce.4
where the time goes:
time: 808 us; the launch traced here: 798 us
  waiting for transfers between devices  289 us (36%)
  matrix products  203 us (25%)
  blocking collectives  133 us (16%)
  local copies, waits for them, and re-layouts  105 us (13%)
  other arithmetic  50.2 us (6%)
  between operations  17 us (2%)
    reduce_scatter x1, waiting for transfers between devices, per_device(): lax.psum_scatter(grads[3], 'fsdp', scatter_dimension=0, tiled=True)  78.4 us
    reduce_scatter x1, waiting for transfers between devices, per_device(): lax.psum_scatter(grads[2], 'fsdp', scatter_dimension=0, tiled=True)  78.2 us
    all_gather x1, blocking collectives, per_device(): piece = lax.all_gather(image_embed, ('fsdp', 'dp'), axis=0, tiled=True)  73.5 us
    psum x1, waiting for transfers between devices, per_device(): lax.psum(owned[0].astype(jnp.bfloat16), 'dp').astype(jnp.float32)  62.4 us
    unnamed x13, waiting for transfers between devices  43.9 us
    dot_general x1, matrix products, forward_block(): jnp.dot(second_low, up_w, preferred_element_type=jnp.float32)  36.2 us
    dot_general x2, matrix products, forward_block(): jnp.dot(active, down_w, preferred_element_type=jnp.float32) + biases[3]  27.3 us
    reduce_scatter x1, waiting for transfers between devices, per_device(): lax.psum_scatter(grads[0], 'fsdp', scatter_dimension=0, tiled=True)  25.8 us
  transfers between devices with their start and end apart: 11, of which 6 were waited for; matrix products, arithmetic and copies ran while one was open for 34% of the time, Pallas kernels for 0%

commit v1 on v0

--- a/solution.py
+++ b/solution.py
@@ -170,6 +170,36 @@
     )
 
 
+def image_first_token(patches, qkv_w, out_w, up_w, down_w, gains_low, biases_low, up_b):
+    rows, length, channel_count = patches.shape
+    gains = gains_low.astype(jnp.float32)
+    biases = biases_low.astype(jnp.float32)
+    heads = channel_count // HEAD_DIM
+    scale = 1.0 / math.sqrt(HEAD_DIM)
+    first_low = layer_norm(patches.astype(jnp.float32), gains[0], biases[4])[0].astype(jnp.bfloat16)
+    flat_low = first_low.reshape(rows * length, channel_count)
+    query = (
+        (jnp.dot(first_low[:, 0], qkv_w[:, :channel_count], preferred_element_type=jnp.float32) + biases[0])
+        * scale
+    ).astype(jnp.bfloat16).reshape(rows, heads, HEAD_DIM)
+    mixed = jnp.dot(flat_low, qkv_w[:, channel_count:], preferred_element_type=jnp.float32)
+    key_low = mixed[:, :channel_count].astype(jnp.bfloat16).reshape(rows, length, heads, HEAD_DIM)
+    value_low = (
+        (mixed[:, channel_count:] + biases[1]).astype(jnp.bfloat16).reshape(rows, length, heads, HEAD_DIM)
+    )
+    scores = jnp.einsum("rhd,rkhd->rhk", query, key_low, preferred_element_type=jnp.float32)
+    probs_low = jax.nn.softmax(scores, axis=-1).astype(jnp.bfloat16)
+    attended = jnp.einsum("rhk,rkhd->rhd", probs_low, value_low, preferred_element_type=jnp.float32)
+    attended = attended.astype(jnp.bfloat16).reshape(rows, channel_count)
+    middle = patches[:, 0].astype(jnp.float32) + (
+        jnp.dot(attended, out_w, preferred_element_type=jnp.float32) + biases[2]
+    )
+    second_low = layer_norm(middle, gains[1], biases[5])[0].astype(jnp.bfloat16)
+    hidden = jnp.dot(second_low, up_w, preferred_element_type=jnp.float32) + up_b.astype(jnp.float32)
+    active = gelu_exact(hidden).astype(jnp.bfloat16)
+    return middle + (jnp.dot(active, down_w, preferred_element_type=jnp.float32) + biases[3])
+
+
 def per_device(
     incoming_word_states,
     sentence_number_per_word,
@@ -203,10 +233,8 @@
         lax.all_gather(widened_offset, "fsdp", axis=0, tiled=True),
     )
     image_rows, image_length = (picture_patches.shape[0], picture_patches.shape[1])
-    image_flat = picture_patches.astype(jnp.float32).reshape(
-        image_rows * image_length, channel_count
-    )
-    image_weights = (
+    image_token = image_first_token(
+        picture_patches,
         picture_lookup_matrices,
         picture_mixer_exit_matrix,
         picture_widening_matrix,
@@ -215,14 +243,12 @@
         picture_offsets,
         picture_widened_offset,
     )
-    image_result = forward_block(image_flat, image_rows, image_length, None, image_weights)[0]
-    image_token = image_result.reshape(image_rows, image_length, channel_count)[:, 0, :]
     image_embed = (
         image_token * lax.rsqrt(jnp.mean(image_token * image_token, axis=-1, keepdims=True) + 1e-06)
     ).astype(jnp.bfloat16)
     mask = sentence_number_per_word[:, :, None] == sentence_number_per_word[:, None, :]
     flat = incoming_word_states.astype(jnp.float32).reshape(rows * length, channel_count)
-    text_result = forward_block(flat, rows, length, mask, whole)[0]
+    text_result, saved = forward_block(flat, rows, length, mask, whole)
     member = (sentence_number_per_word[:, :, None] == jnp.arange(CAPS, dtype=jnp.int32)).astype(
         jnp.float32
     )
@@ -262,35 +288,21 @@
     token_grad = jnp.einsum(
         "rsc,rcd->rsd", member, per_caption, precision=lax.Precision.HIGHEST
     ).reshape(rows * length, channel_count)
-    again = (
-        lax.all_gather(lookup_matrices, "fsdp", axis=0, tiled=True),
-        lax.all_gather(mixer_exit_matrix, "fsdp", axis=0, tiled=True),
-        lax.all_gather(widening_matrix, "fsdp", axis=0, tiled=True),
-        lax.all_gather(narrowing_matrix, "fsdp", axis=0, tiled=True),
-        lax.all_gather(normalizer_multipliers, "fsdp", axis=1, tiled=True),
-        lax.all_gather(word_offsets, "fsdp", axis=1, tiled=True),
-        lax.all_gather(widened_offset, "fsdp", axis=0, tiled=True),
-    )
-    saved = forward_block(flat, rows, length, mask, again)[1]
-    input_grad, grads = backward_block(token_grad, saved, again, rows, length)
-    owned = (
-        lax.psum_scatter(grads[0], "fsdp", scatter_dimension=0, tiled=True),
-        lax.psum_scatter(grads[1], "fsdp", scatter_dimension=0, tiled=True),
-        lax.psum_scatter(grads[2], "fsdp", scatter_dimension=0, tiled=True),
-        lax.psum_scatter(grads[3], "fsdp", scatter_dimension=0, tiled=True),
-        lax.psum_scatter(grads[4], "fsdp", scatter_dimension=1, tiled=True),
-        lax.psum_scatter(grads[5], "fsdp", scatter_dimension=1, tiled=True),
-        lax.psum_scatter(grads[6], "fsdp", scatter_dimension=0, tiled=True),
-    )
-    summed = (
-        lax.psum(owned[0].astype(jnp.bfloat16), "dp").astype(jnp.float32),
-        lax.psum(owned[1].astype(jnp.bfloat16), "dp").astype(jnp.float32),
-        lax.psum(owned[2].astype(jnp.bfloat16), "dp").astype(jnp.float32),
-        lax.psum(owned[3].astype(jnp.bfloat16), "dp").astype(jnp.float32),
-        lax.psum(owned[4].astype(jnp.bfloat16), "dp").astype(jnp.float32),
-        lax.psum(owned[5].astype(jnp.bfloat16), "dp").astype(jnp.float32),
-        lax.psum(owned[6].astype(jnp.bfloat16), "dp").astype(jnp.float32),
-    )
+    input_grad, grads = backward_block(token_grad, saved, whole, rows, length)
+    owned = [
+        lax.psum(
+            lax.psum_scatter(piece_grad.astype(jnp.bfloat16), "fsdp", scatter_dimension=0, tiled=True), "dp"
+        ).astype(jnp.float32)
+        for piece_grad in grads[:4]
+    ]
+    small = jnp.concatenate([grads[4], grads[5], grads[6].reshape(-1, channel_count)], axis=0)
+    small = lax.psum(small, ("fsdp", "dp"))
+    place = lax.axis_index("fsdp")
+    width = normalizer_multipliers.shape[1]
+    columns = lax.dynamic_slice_in_dim(small[:8], place * width, width, axis=1)
+    hidden_width = widened_offset.shape[0]
+    hidden_part = lax.dynamic_slice_in_dim(small[8:].reshape(-1), place * hidden_width, hidden_width)
+    summed = (*owned, columns[:2], columns[2:8], hidden_part)
     grad_input = input_grad.astype(jnp.bfloat16).reshape(rows, length, channel_count)
     return (
         summed[0],

time: 808 us -> 633 us (0.78)
  waiting for transfers between devices: 289 us -> 176 us
  matrix products: 203 us -> 171 us
  local copies, waits for them, and re-layouts: 105 us -> 83.4 us
  other arithmetic: 50.2 us -> 37.2 us
    psum x1, waiting for transfers between devices: 62.4 us -> 20.9 us  [per_device(): lax.psum(lax.psum_scatter(piece_grad.astype(jnp.bfloat16), 'fsdp', scatte...]
    unnamed x13 -> x9, waiting for transfers between devices: 43.9 us -> 2.66 us
    reduce_scatter x4, waiting for transfers between devices: 182 us -> 153 us  [per_device(): lax.psum_scatter(piece_grad.astype(jnp.bfloat16), 'fsdp', scatter_dimensi...]
    psum x1, blocking collectives: 12.5 us -> 41.4 us  [per_device(): small = lax.psum(small, ('fsdp', 'dp'))]
    unnamed x1 -> x0, blocking collectives: 22.9 us -> none
    dot_general x2 -> x1, matrix products: 27.3 us -> 9.19 us  [forward_block(): jnp.dot(active, down_w, preferred_element_type=jnp.float32) + biases[3]]
    dot_general x0 -> x6, matrix products: none -> 14.7 us  [the longest x1 5.47 us: image_first_token(): jnp.dot(active, down_w, preferred_element_type=jnp.float32) + biases[3]]
    convert_element_type x11 -> x9, other arithmetic: 17.1 us -> 8.6 us  [the longest x4 6.1 us: per_device(): owned = [lax.psum(lax.psum_scatter(piece_grad.astype(jnp.bfloat16), 'fsdp...]
  transfers between devices with their start and end apart: 11 -> 9, of which waited for: 6 -> 4; matrix products, arithmetic and copies ran while one was open for 34% -> 30% of each run, Pallas kernels for 0% -> 0%
where the time goes in v1:
time: 633 us; the launch traced here: 625 us
  waiting for transfers between devices  176 us (28%)
  matrix products  171 us (27%)
  blocking collectives  140 us (22%)
  local copies, waits for them, and re-layouts  83.4 us (13%)
  other arithmetic  37.2 us (6%)
  between operations  16.3 us (3%)
    reduce_scatter x4, waiting for transfers between devices, per_device(): lax.psum_scatter(piece_grad.astype(jnp.bfloat16), 'fsdp', scatter_dimensi...  153 us
    all_gather x1, blocking collectives, per_device(): piece = lax.all_gather(image_embed, ('fsdp', 'dp'), axis=0, tiled=True)  73.4 us
    psum x1, blocking collectives, per_device(): small = lax.psum(small, ('fsdp', 'dp'))  41.4 us
    dot_general x1, matrix products, forward_block(): jnp.dot(second_low, up_w, preferred_element_type=jnp.float32)  38.3 us
    psum x1, waiting for transfers between devices, per_device(): lax.psum(lax.psum_scatter(piece_grad.astype(jnp.bfloat16), 'fsdp', scatte...  20.9 us
    dot_general x1, matrix products, backward_block(): jnp.einsum('nd,fd->nf', down_grad, down_w, preferred_element_type=jnp.flo...  17 us
  transfers between devices with their start and end apart: 9, of which 4 were waited for; matrix products, arithmetic and copies ran while one was open for 30% of the time, Pallas kernels for 0%

profile of v1, /device:TPU:0, one launch (start us, length us, event | category | flops | bytes accessed | tf_op | source)
XLA Modules:
  0.0 625.3 jit_solution(15457575982006405987)
XLA Ops:
  20.2 3.1 fusion.32
  25.7 3.0 reshape.225
  28.7 2.2 fusion.48
  33.4 3.1 reshape.226
  39.2 5.5 multiply_reduce_fusion.8
  44.8 73.4 %all_gather.31 = bf16[256,768]{1,0:T(8,128)(2,1)S(1)} all-gather(bf16[8,768]{1,0:T(8,128)(2,1)S(1)} %multiply_convert_fusion.6), channel_id=1, replica_groups=mesh['fsdp'=8,'dp'=4] {'fsdp','dp'}, dimensions={0}, use_global_device_ids=true | all-gather | bytes 405504 | tf_op jit(solution)/shard_map/all_gather | solution.py:270
  118.2 7.9 %all-gather.1 = bf16[8,96,6]{1,2,0:T(8,128)(2,1)S(1)} all-gather(bf16[1,96,6]{1,2,0:T(8,128)(2,1)S(1)} %bitcast.132), channel_id=1, replica_groups=mesh['fsdp'=8,'dp'=4] {'fsdp'}, dimensions={0}, use_global_device_ids=true | all-gather | bytes 10368 | tf_op jit(solution)/shard_map/all_gather | solution.py:232
  126.9 8.9 %all-gather = bf16[8,96,2]{1,2,0:T(2,128)(2,1)S(1)} all-gather(bf16[1,96,2]{1,2,0:T(2,128)(2,1)S(1)} %bitcast.133), channel_id=1, replica_groups=mesh['fsdp'=8,'dp'=4] {'fsdp'}, dimensions={0}, use_global_device_ids=true | all-gather | bytes 3456 | tf_op jit(solution)/shard_map/all_gather | solution.py:231
  136.6 8.3 %all-gather.2 = bf16[8,1,384]{2,1,0:T(2,128)(2,1)S(1)} all-gather(bf16[1,1,384]{2,1,0:T(2,128)(2,1)S(1)} %reshape.241), channel_id=1, replica_groups=mesh['fsdp'=8,'dp'=4] {'fsdp'}, dimensions={0}, use_global_device_ids=true | all-gather | bytes 6912 | tf_op jit(solution)/shard_map/all_gather | solution.py:233
  148.6 6.3 %fusion.178 = f32[1024,2304]{1,0:T(8,128)S(1)} fusion(bf16[1024,768]{1,0:T(8,128)(2,1)} %fusion.23, bf16[768,2304]{1,0:T(8,128)(2,1)} %all-gather.8.cloned.1.call-done), kind=kOutput, calls=%fused_computation.283 | convolution fusion | flops 3623878656 | bytes 14548992 | tf_op jit(solution)/shard_map/dot_general | solution.py:38
  158.0 3.9 reshape.270
  161.9 6.4 %copy.123 = bf16[16,64,12,64]{1,3,2,0:T(8,128)(2,1)S(1)} copy(bf16[16,64,12,64]{3,2,1,0:T(8,128)(2,1)} %reshape.270) | data formatting | bytes 3145728 | tf_op jit(solution)/shard_map/reshape | solution.py:42
  168.3 6.2 reshape.252
  174.5 5.9 reshape.271
  180.4 3.2 fusion.39
  183.6 2.2 fusion.173
  188.6 4.2 copy.115
  192.7 4.6 reshape.220
  197.4 5.0 fusion.174
  202.4 2.4 multiply_reduce_fusion.3
  204.8 38.3 %multiply_convert_fusion = (bf16[1024,3072]{1,0:T(8,128)(2,1)}, f32[1024,3072]{1,0:T(8,128)}, f32[1024,3072]{1,0:T(8,128)}) fusion(f32[3072]{0:T(1024)S(1)} %bitcast.130, bf16[768,3072]{1,0:T(8,128)(2,1)} %all-gather.12.cloned.1.call-done, f32[1024,768]{1,0:T(8,128)} %get-tuple-element.48, f32[768]{0:T(1024)S(1)} %copy-done.46, f32[768]{0:T(1024)S(1)} %copy-done.38, ...), kind=kOutput, calls=%fused_computation.7 | convolution fusion | flops 5043388416 | bytes 39348224 | tf_op jit(solution)/shard_map/dot_general | solution.py:66
  243.2 9.2 %add_add_fusion = f32[1024,768]{1,0:T(8,128)S(1)} fusion(f32[1024,768]{1,0:T(8,128)} %get-tuple-element.48, bf16[1024,3072]{1,0:T(8,128)(2,1)} %get-tuple-element.39, bf16[3072,768]{1,0:T(8,128)(2,1)} %all-gather.14.cloned.1.call-done, f32[768]{0:T(1024)S(1)} %copy-done.48), kind=kOutput, calls=%fused_computation.66 | convolution fusion | flops 4833411072 | bytes 17304576 | tf_op jit(solution)/shard_map/dot_general | solution.py:70
  257.6 17.0 %convert_reduce_fusion = (f32[3072]{0:T(1024)S(1)}, bf16[1024,3072]{1,0:T(8,128)(2,1)}) fusion(f32[1024,3072]{1,0:T(8,128)} %get-tuple-element.40, bf16[1024,768]{1,0:T(8,128)(2,1)S(1)} %get-tuple-element.44, bf16[3072,768]{1,0:T(8,128)(2,1)} %all-gather.14.cloned.1.call-done, f32[1024,3072]{1,0:T(8,128)} %get-tuple-element.49, f32[3072]{0:T(1024)S(1)} %bitcast.131), kind=kOutput, calls=%fused_computation.5 | convolution fusion | flops 4885312512 | bytes 37773312 | tf_op jit(solution)/shard_map/nd,fd->nf/dot_general | solution.py:116
  274.6 9.7 %multiply_reduce_fusion.1 = (f32[768]{0:T(1024)S(1)}, f32[1024]{0:T(1024)S(1)}, f32[1024]{0:T(1024)S(1)}, f32[768]{0:T(1024)S(1)}, f32[1024,768]{1,0:T(8,128)S(1)}) fusion(f32[1024,768]{1,0:T(8,128)} %get-tuple-element.48, f32[1024]{0:T(1024)S(1)} %add_rsqrt_fusion.3, f32[1024]{0:T(1024)S(1)} %broadcast_multiply_fusion.6, f32[768]{0:T(1024)S(1)} %copy-done.38, ...), kind=kOutput, calls=%fused_computation.61 | convolution fusion | flops 4838912000 | bytes 17327104 | tf_op jit(solution)/shard_map/nf,df->nd/dot_general | solution.py:121
  284.4 2.8 convert_reduce_fusion.5
  287.2 2.6 convolution_convert_fusion.3
  289.8 6.1 reshape.253
  295.9 7.4 %convert_reduce_fusion.1 = (f32[12,64]{1,0:T(8,128)S(1)}, bf16[16,64,12,64]{3,1,2,0:T(8,128)(2,1)}) fusion(bf16[16,64,12,64]{3,2,1,0:T(8,128)(2,1)} %reshape.253, f32[16,12,64,64]{2,3,1,0:T(8,128)} %copy-done.11, f32[16,12,64]{2,1,0:T(8,128)S(1)} %copy-done.27), kind=kOutput, calls=%fused_computation.21 | convolution fusion | flops 104594688 | bytes 6343680 | tf_op jit(solution)/shard_map/rhqk,rqhd->rkhd/dot_general | solution.py:133
  303.4 5.9 multiply_reduce_fusion
  309.2 2.4 convolution_convert_fusion.4
  311.7 4.2 copy.127
  315.9 3.2 reshape.232
  319.1 6.8 %multiply_convert_fusion.1 = bf16[16,12,64,64]{2,3,1,0:T(8,128)(2,1)S(1)} fusion(f32[16,12,64,64]{2,3,1,0:T(8,128)} %get-tuple-element.60, f32[16,12,64]{2,1,0:T(8,128)S(1)} %get-tuple-element.59, f32[16,12,64,64]{2,3,1,0:T(8,128)} %copy-done.11, f32[16,12,64]{2,1,0:T(8,128)S(1)} %copy-done.27), kind=kLoop, calls=%fused_computation.23 | loop fusion | flops 3145728 | bytes 7962624 | tf_op jit(solution)/shard_map/convert_element_type | solution.py:137
  327.6 2.4 copy.125
  330.1 3.2 reshape.231
  333.7 6.7 %convert_reduce_fusion.2 = (f32[12,64]{1,0:T(8,128)S(1)}, bf16[16,12,64,64]{2,3,1,0:T(8,128)(2,1)}) fusion(bf16[16,12,64,64]{2,3,1,0:T(8,128)(2,1)} %copy-done.8, bf16[16,64,12,64]{3,2,1,0:T(8,128)(2,1)} %reshape.252), kind=kOutput, calls=%fused_computation.22 | convolution fusion | flops 103808256 | bytes 4721664 | tf_op jit(solution)/shard_map/rhqk,rkhd->rqhd/dot_general | solution.py:138
  340.4 4.3 copy.122
  344.7 3.2 mul.341
  352.5 5.4 convolution_convert_fusion.2
  359.3 9.8 %convolution_convert_fusion = bf16[3072,768]{1,0:T(8,128)(2,1)} fusion(bf16[1024,3072]{1,0:T(8,128)(2,1)} %get-tuple-element.39, bf16[1024,768]{1,0:T(8,128)(2,1)S(1)} %copy-done.20), kind=kOutput, calls=%fused_computation.28 | convolution fusion | flops 4834197504 | bytes 12582912 | tf_op jit(solution)/shard_map/nf,nd->fd/dot_general | solution.py:115
  369.7 10.4 %convolution_convert_fusion.1 = bf16[768,3072]{1,0:T(8,128)(2,1)} fusion(bf16[1024,3072]{1,0:T(8,128)(2,1)} %get-tuple-element.67, f32[1024,768]{1,0:T(8,128)} %get-tuple-element.48, f32[768]{0:T(1024)S(1)} %copy-done.47, f32[768]{0:T(1024)S(1)} %copy-done.39, f32[1024]{0:T(1024)S(1)} %copy-done.41, f32[1024]{0:T(1024)S(1)} %copy-done.36), kind=kOutput, calls=%fused_computation.29 | convolution fusion | flops 4838129664 | bytes 14170112 | tf_op jit(solution)/shard_map/nd,nf->df/dot_general | solution.py:120
  380.5 38.3 %reduce-scatter.5.cloned.1.call-done = bf16[96,2304]{1,0:T(8,128)(2,1)} async-done(((bf16[768,2304]{1,0:T(8,128)(2,1)}), bf16[96,2304]{1,0:T(8,128)(2,1)}) %reduce-scatter.5.cloned.1.call-update) | async-done | bytes 442384 | tf_op jit(solution)/shard_map/reduce_scatter | solution.py:294
  418.8 57.3 %reduce-scatter.11.cloned.1.call-done = bf16[384,768]{1,0:T(8,128)(2,1)} async-done(((bf16[3072,768]{1,0:T(8,128)(2,1)}), bf16[384,768]{1,0:T(8,128)(2,1)}) %reduce-scatter.11.cloned.1.call-update) | async-done | bytes 589840 | tf_op jit(solution)/shard_map/reduce_scatter | solution.py:294
  476.1 57.3 %reduce-scatter.9.cloned.1.call-done = bf16[96,3072]{1,0:T(8,128)(2,1)} async-done(((bf16[768,3072]{1,0:T(8,128)(2,1)}), bf16[96,3072]{1,0:T(8,128)(2,1)}) %reduce-scatter.9.cloned.1.call-update) | async-done | bytes 589840 | tf_op jit(solution)/shard_map/reduce_scatter | solution.py:294
  533.4 9.6 %fusion.25 = (f32[1024]{0:T(1024)S(1)}, f32[768]{0:T(1024)S(1)}, f32[1024]{0:T(1024)S(1)}, f32[768]{0:T(1024)S(1)}, f32[1024,768]{1,0:T(8,128)}) fusion(bf16[16,64,768]{2,1,0:T(8,128)(2,1)S(1)} %copy-done.6, f32[768]{0:T(1024)S(1)} %copy-done.34, f32[1024]{0:T(1024)S(1)} %copy-done.32, f32[1024]{0:T(1024)S(1)} %copy-done.30, ...), kind=kOutput, calls=%fused_computation.54 | convolution fusion | flops 3631739392 | bytes 13001728 | tf_op jit(solution)/shard_map/ne,de->nd/dot_general | solution.py:152
  543.3 41.4 %psum.39 = f32[12,768]{1,0:T(8,128)S(1)} all-reduce(f32[12,768]{1,0:T(8,128)S(1)} %concatenate.7), channel_id=1, replica_groups=mesh['fsdp'=8,'dp'=4] {'fsdp','dp'}, use_global_device_ids=true, to_apply=%region_36.37 | all-reduce | flops 9216 | bytes 73728 | tf_op jit(solution)/shard_map/psum | solution.py:299
  587.2 4.4 fusion.29
  591.6 20.9 %all-reduce.3.cloned.1.call-done = (bf16[96,2304]{1,0:T(8,128)(2,1)}, bf16[96,768]{1,0:T(8,128)(2,1)}, bf16[96,3072]{1,0:T(8,128)(2,1)}, bf16[384,768]{1,0:T(8,128)(2,1)}) async-done(((bf16[96,2304]{1,0:T(8,128)(2,1)}, bf16[96,768]{1,0:T(8,128)(2,1)}, bf16[96,3072]{1,0:T(8,128)(2,1)}, bf16[384,768]{1,0:T(8,128)(2,1)}), (bf16[96,2304]{1,0:T(8,128)(2,1)}, bf16[96,768]{1,0:T(8,128)(2,1)}, ...) | async-done | bytes 1769488 | tf_op jit(solution)/shard_map/psum | solution.py:293
  (223 shorter events, 53.2 us)
Async XLA Ops:
  7.2 31.3 %copy-start = (bf16[768,768]{1,0:T(8,128)(2,1)S(1)}, bf16[768,768]{1,0:T(8,128)(2,1)}, u32[]{:S(2)}) copy-start(bf16[768,768]{1,0:T(8,128)(2,1)} %param.32) | copy-start | bytes 3538948
  7.2 4.6 copy-start.4
  7.2 6.4 %copy-start.24 = (s32[16,64]{1,0:T(8,128)S(1)}, s32[16,64]{1,0:T(8,128)}, u32[]{:S(2)}) copy-start(s32[16,64]{1,0:T(8,128)} %param.21) | copy-start | bytes 12292
  7.2 7.3 %copy-start.44 = (bf16[6,768]{1,0:T(8,128)(2,1)S(1)}, bf16[6,768]{1,0:T(8,128)(2,1)}, u32[]{:S(2)}) copy-start(bf16[6,768]{1,0:T(8,128)(2,1)} %param.36) | copy-start | bytes 27652
  7.2 7.4 %copy-start.49 = (bf16[2,768]{1,0:T(2,128)(2,1)S(1)}, bf16[2,768]{1,0:T(2,128)(2,1)}, u32[]{:S(2)}) copy-start(bf16[2,768]{1,0:T(2,128)(2,1)} %param.35) | copy-start | bytes 9220
  7.2 7.4 %copy-start.12 = (bf16[8,50,768]{2,0,1:T(8,128)(2,1)S(1)}, bf16[8,50,768]{2,0,1:T(8,128)(2,1)}, u32[]{:S(2)}) copy-start(bf16[8,50,768]{2,0,1:T(8,128)(2,1)} %param.30) | copy-start | bytes 1843204
  7.2 141.3 %all-gather.8.cloned.1.call-start = ((), (), s32[]{:S(2)}) async-start(), calls=%async_computation.4 | async-start | bytes 3981312 | tf_op jit(solution)/shard_map/all_gather | solution.py:227
  8.0 189.4 %all-gather.10.cloned.1.call-start = ((), (), s32[]{:S(2)}) async-start(), calls=%async_computation.5 | async-start | bytes 1327104 | tf_op jit(solution)/shard_map/all_gather | solution.py:228
  8.7 196.1 %all-gather.12.cloned.1.call-start = ((), (), s32[]{:S(2)}) async-start(), calls=%async_computation.6 | async-start | bytes 5308416 | tf_op jit(solution)/shard_map/all_gather | solution.py:229
  9.5 233.7 %all-gather.14.cloned.1.call-start = ((), (), s32[]{:S(2)}) async-start(), calls=%async_computation.7 | async-start | bytes 5308416 | tf_op jit(solution)/shard_map/all_gather | solution.py:230
  10.0 370.4 %reduce-scatter.7.cloned.1.call-start = ((), (), s32[]{:S(2)}) async-start(), calls=%async_computation.9 | async-start | bytes 1327104 | tf_op jit(solution)/shard_map/reduce_scatter | solution.py:294
  31.2 7.9 %copy-start.45 = (bf16[3072]{0:T(1024)(128)(2,1)S(1)}, bf16[3072]{0:T(1024)(128)(2,1)}, u32[]{:S(2)}) copy-start(bf16[3072]{0:T(1024)(128)(2,1)} %param.37) | copy-start | bytes 18436
  39.1 79.1 %copy-start.50 = (bf16[6,96]{1,0:T(8,128)(2,1)S(1)}, bf16[6,96]{1,0:T(8,128)(2,1)}, u32[]{:S(2)}) copy-start(bf16[6,96]{1,0:T(8,128)(2,1)} %param.28) | copy-start | bytes 3460
  39.2 87.7 %copy-start.37 = (f32[16,64]{1,0:T(8,128)S(1)}, f32[16,64]{1,0:T(8,128)}, u32[]{:S(2)}) copy-start(f32[16,64]{1,0:T(8,128)} %fusion.16) | copy-start | bytes 12292
  39.2 87.8 %copy-start.53 = (bf16[2,96]{1,0:T(2,128)(2,1)S(1)}, bf16[2,96]{1,0:T(2,128)(2,1)}, u32[]{:S(2)}) copy-start(bf16[2,96]{1,0:T(2,128)(2,1)} %param.27) | copy-start | bytes 1156
  39.2 97.4 %copy-start.52 = (bf16[384]{0:T(512)(128)(2,1)S(1)}, bf16[384]{0:T(512)(128)(2,1)}, u32[]{:S(2)}) copy-start(bf16[384]{0:T(512)(128)(2,1)} %param.29) | copy-start | bytes 2308
  39.2 107.6 %copy-start.29 = (f32[1024]{0:T(1024)S(1)}, f32[1024]{0:T(1024)}, u32[]{:S(2)}) copy-start(f32[1024]{0:T(1024)} %div.92) | copy-start | bytes 12292
  126.9 28.0 %copy-start.31 = (f32[1024]{0:T(1024)}, f32[1024]{0:T(1024)S(1)}, u32[]{:S(2)}) copy-start(f32[1024]{0:T(1024)S(1)} %rsqrt.55) | copy-start | bytes 12292
  136.6 18.4 %copy-start.33 = (f32[768]{0:T(1024)}, f32[768]{0:T(1024)S(1)}, u32[]{:S(2)}) copy-start(f32[768]{0:T(1024)S(1)} %get-tuple-element.30) | copy-start | bytes 9220
  168.3 12.1 %copy-start.2 = (bf16[16,64,12,64]{1,3,2,0:T(8,128)(2,1)}, bf16[16,64,12,64]{1,3,2,0:T(8,128)(2,1)S(1)}, u32[]{:S(2)}) copy-start(bf16[16,64,12,64]{1,3,2,0:T(8,128)(2,1)S(1)} %copy.123) | copy-start | bytes 4718596
  180.4 3.2 copy-start.28
  192.7 4.6 copy-start.5
  197.3 5.0 copy-start.17
  202.4 72.2 %copy-start.35 = (f32[1024]{0:T(1024)}, f32[1024]{0:T(1024)S(1)}, u32[]{:S(2)}) copy-start(f32[1024]{0:T(1024)S(1)} %broadcast_multiply_fusion.6) | copy-start | bytes 12292
  204.8 69.8 %copy-start.40 = (f32[1024]{0:T(1024)}, f32[1024]{0:T(1024)S(1)}, u32[]{:S(2)}) copy-start(f32[1024]{0:T(1024)S(1)} %add_rsqrt_fusion.3) | copy-start | bytes 12292
  204.8 38.3 %copy-start.48 = (f32[768]{0:T(1024)S(1)}, f32[768]{0:T(1024)}, u32[]{:S(2)}) copy-start(f32[768]{0:T(1024)} %get-tuple-element.17) | copy-start | bytes 9220
  257.3 17.3 %copy-start.19 = (bf16[1024,768]{1,0:T(8,128)(2,1)}, bf16[1024,768]{1,0:T(8,128)(2,1)S(1)}, u32[]{:S(2)}) copy-start(bf16[1024,768]{1,0:T(8,128)(2,1)S(1)} %get-tuple-element.44) | copy-start | bytes 4718596
  274.6 9.8 %copy-start.39 = (f32[768]{0:T(1024)S(1)}, f32[768]{0:T(1024)}, u32[]{:S(2)}) copy-start(f32[768]{0:T(1024)} %get-tuple-element.29) | copy-start | bytes 9220
  284.4 2.8 copy-start.55
  287.2 22.1 %copy-start.7 = (f32[1024,768]{1,0:T(8,128)}, f32[1024,768]{1,0:T(8,128)S(1)}, u32[]{:S(2)}) copy-start(f32[1024,768]{1,0:T(8,128)S(1)} %get-tuple-element.38) | copy-start | bytes 9437188
  289.8 6.1 copy-start.27
  295.9 7.4 %copy-start.14 = (bf16[16,64,12,64]{3,2,1,0:T(8,128)(2,1)S(1)}, bf16[16,64,12,64]{3,2,1,0:T(8,128)(2,1)}, u32[]{:S(2)}) copy-start(bf16[16,64,12,64]{3,2,1,0:T(8,128)(2,1)} %reshape.271) | copy-start | bytes 4718596
  295.9 7.4 %copy-start.15 = (bf16[16,64,12,64]{3,2,1,0:T(8,128)(2,1)S(1)}, bf16[16,64,12,64]{3,2,1,0:T(8,128)(2,1)}, u32[]{:S(2)}) copy-start(bf16[16,64,12,64]{3,2,1,0:T(8,128)(2,1)} %reshape.253) | copy-start | bytes 4718596
  303.3 5.9 copy-start.18
  319.1 6.8 %copy-start.3 = (bf16[16,64,12,64]{1,3,2,0:T(8,128)(2,1)S(1)}, bf16[16,64,12,64]{1,3,2,0:T(8,128)(2,1)}, u32[]{:S(2)}) copy-start(bf16[16,64,12,64]{1,3,2,0:T(8,128)(2,1)} %copy-done.2) | copy-start | bytes 4718596
  333.3 85.5 %reduce-scatter.5.cloned.1.call-start = ((), (), s32[]{:S(2)}) async-start(), calls=%async_computation.8 | async-start | bytes 3981312 | tf_op jit(solution)/shard_map/reduce_scatter | solution.py:294
  349.7 2.7 copy-start.16
  357.9 118.1 %reduce-scatter.11.cloned.1.call-start = ((), (), s32[]{:S(2)}) async-start(), calls=%async_computation.11 | async-start | bytes 5308416 | tf_op jit(solution)/shard_map/reduce_scatter | solution.py:294
  369.1 164.2 %reduce-scatter.9.cloned.1.call-start = ((), (), s32[]{:S(2)}) async-start(), calls=%async_computation.10 | async-start | bytes 5308416 | tf_op jit(solution)/shard_map/reduce_scatter | solution.py:294
  380.2 153.2 %copy-start.6 = (bf16[16,64,768]{2,1,0:T(8,128)(2,1)S(1)}, bf16[16,64,768]{2,1,0:T(8,128)(2,1)}, u32[]{:S(2)}) copy-start(bf16[16,64,768]{2,1,0:T(8,128)(2,1)} %param.20) | copy-start | bytes 4718596
  380.2 153.2 %copy-start.30 = (f32[1024]{0:T(1024)S(1)}, f32[1024]{0:T(1024)}, u32[]{:S(2)}) copy-start(f32[1024]{0:T(1024)} %div.92) | copy-start | bytes 12292
  380.2 153.2 %copy-start.32 = (f32[1024]{0:T(1024)S(1)}, f32[1024]{0:T(1024)}, u32[]{:S(2)}) copy-start(f32[1024]{0:T(1024)} %copy-done.31) | copy-start | bytes 12292
  380.2 153.2 %copy-start.34 = (f32[768]{0:T(1024)S(1)}, f32[768]{0:T(1024)}, u32[]{:S(2)}) copy-start(f32[768]{0:T(1024)} %copy-done.33) | copy-start | bytes 9220
  380.2 232.3 %all-reduce.3.cloned.1.call-start = ((), (), s32[]{:S(2)}) async-start(), calls=%async_computation.12 | async-start | bytes 3538944 | tf_op jit(solution)/shard_map/psum | solution.py:293
  533.4 53.3 %copy-start.54 = (f32[64]{0:T(128)S(1)}, f32[64]{0:T(128)}, u32[]{:S(2)}) copy-start(f32[64]{0:T(128)} %get-tuple-element.68) | copy-start | bytes 772
  587.2 31.4 %copy-start.1 = (bf16[768,768]{1,0:T(8,128)(2,1)S(1)}, bf16[768,768]{1,0:T(8,128)(2,1)}, u32[]{:S(2)}) copy-start(bf16[768,768]{1,0:T(8,128)(2,1)} %param.32) | copy-start | bytes 3538948
  612.5 4.4 copy-start.23
  612.5 5.4 copy-start.25
  (17 other events, 30.2 us)
Sparse Core Ops, SparseCore 0:
  9.9 36.5 all-gather.7
  48.4 24.1 all-gather.9
  74.5 39.5 all-gather.11
  115.8 38.5 all-gather.13
  333.4 34.0 reduce-scatter.6
  370.8 47.9 reduce-scatter.4
  422.2 53.7 reduce-scatter.10
  479.5 53.7 reduce-scatter.8
  536.0 76.5 all-reduce.2

commit v2 on v1

--- a/solution.py
+++ b/solution.py
@@ -3,6 +3,8 @@
 import jax
 import jax.numpy as jnp
 from jax import lax
+from jax.experimental import pallas as pl
+from jax.experimental.pallas import tpu as pltpu
 from jax.sharding import PartitionSpec as P
 
 HEAD_DIM = 64
@@ -317,9 +319,1145 @@
     )
 
 
+BF = jnp.bfloat16
+F32 = jnp.float32
+MESH_ID = pl.DeviceIdType.MESH
+TILE = 256
+N_AG = 11
+D_UNIT = 8
+
+
+def nn(a, b):
+    return jnp.dot(a, b, preferred_element_type=F32)
+
+
+def nt(a, b):
+    return lax.dot_general(a, b, (((1,), (1,)), ((), ())), preferred_element_type=F32)
+
+
+def tn(a, b):
+    return lax.dot_general(a, b, (((0,), (0,)), ((), ())), preferred_element_type=F32)
+
+
+def span(start, size, unit=16):
+    if isinstance(start, int):
+        return pl.ds(start, size)
+    return pl.ds(pl.multiple_of(start, unit), size)
+
+
+def norm_rows(values):
+    centred = values - jnp.mean(values, axis=-1, keepdims=True)
+    inverse = lax.rsqrt(jnp.mean(centred * centred, axis=-1, keepdims=True) + 1e-06)
+    return centred * inverse, inverse
+
+
+def normal_cdf(values):
+    return 0.5 * (1.0 + lax.erf(values * math.sqrt(0.5)))
+
+
+def loop(count, body, events=None):
+    def step(i, carry):
+        body(i)
+        for at, calls in (events or {}).items():
+
+            @pl.when(i == at)
+            def _(calls=calls):
+                for call in calls:
+                    call()
+
+        return carry
+
+    lax.fori_loop(0, count, step, 0)
+
+
+def fused_kernel(
+    sharp_ref,
+    offset_ref,
+    x_hbm,
+    caprow_ref,
+    described_ref,
+    qkv_hbm,
+    out_hbm,
+    up_hbm,
+    down_hbm,
+    small_hbm,
+    patches_ref,
+    pqkv_hbm,
+    pout_hbm,
+    pup_hbm,
+    pdown_hbm,
+    psmall_ref,
+    units_out,
+    down_out,
+    input_out,
+    small_out,
+    loss_out,
+    wts,
+    wdn,
+    h1,
+    qkv,
+    att,
+    x1,
+    h2,
+    act,
+    dg,
+    gm,
+    sdn,
+    lc,
+    lcd,
+    lx,
+    lxd,
+    ly,
+    lyd,
+    lz,
+    lzd,
+    work,
+    faces,
+    small_in,
+    params,
+    member,
+    pooled,
+    caption_hi,
+    caption_lo,
+    partial,
+    small_sum,
+    small_land,
+    face_rows,
+    ag_send,
+    ag_recv,
+    core_send,
+    core_recv,
+    xy_send,
+    xy_recv,
+    z_send,
+    z_recv,
+    side_send,
+    side_recv,
+    local_sem,
+):
+    fs = lax.axis_index("fsdp")
+    dp = lax.axis_index("dp")
+    core = fs % 2
+    xb = (fs // 2) % 2
+    yb = fs // 4
+    fs_core = fs + 1 - 2 * core
+    fs_x = fs + 2 - 4 * xb
+    fs_y = fs + 4 - 8 * yb
+    fs_diag = fs_x + 4 - 8 * yb
+    flip = 1 - 2 * core
+    peer_core = (fs_core, dp)
+    peer_x = (fs_x, dp)
+    peer_y = (fs_y, dp)
+    half_z = dp // 2
+    is_end = (dp == 0) | (dp == 3)
+    is_mid = (dp == 1) | (dp == 2)
+    near = half_z
+    far = 1 - half_z
+    dp_inner = 1 + half_z
+    dp_end = 3 * half_z
+    dp_mid = 2 - half_z
+    dp_pair = dp + 1 - 2 * (dp % 2)
+    dp_far = dp + 2 - 4 * half_z
+
+    barrier = pltpu.get_barrier_semaphore()
+    greet = [peer_core, peer_x, peer_y, (fs, dp_pair), (fs, dp_far)]
+    for peer in greet:
+        pl.semaphore_signal(barrier, inc=1, device_id=peer, device_id_type=MESH_ID)
+
+    local = []
+
+    def fetch(src, dst):
+        copy = pltpu.make_async_copy(src, dst, local_sem.at[len(local)])
+        copy.start()
+        local.append(copy)
+        return copy
+
+    own_rows = span(96 * fs, 96)
+    own_copies = [fetch(qkv_hbm.at[:, pl.ds(768 * j, 768)], wts.at[j, own_rows, :]) for j in range(3)]
+    own_copies.append(fetch(out_hbm, wts.at[3, own_rows, :]))
+    own_copies += [fetch(up_hbm.at[:, pl.ds(768 * j, 768)], wts.at[4 + j, own_rows, :]) for j in range(4)]
+    own_copies.append(fetch(down_hbm, wdn.at[span(384 * fs, 384), :]))
+    small_copy = fetch(small_hbm, small_in.at[fs])
+    pqkv_copy = fetch(pqkv_hbm, act.at[pl.ds(0, 768), pl.ds(0, 2304)])
+    x_copy = fetch(x_hbm, h2)
+    pout_copy = fetch(pout_hbm, act.at[pl.ds(0, 768), pl.ds(2304, 768)])
+    pup_copy = fetch(pup_hbm, dg.at[pl.ds(0, 768), :])
+    pdown_copy = fetch(pdown_hbm, sdn)
+
+    pl.semaphore_wait(barrier, len(greet))
+
+    def weight(unit, shard, part=None):
+        if unit < 8:
+            rows = span(96 * shard, 96) if part is None else span(96 * shard + 48 * part, 48)
+            return wts.at[unit, rows, :]
+        rows = span(384 * shard, 384) if part is None else span(384 * shard + 192 * part, 192)
+        return wdn.at[rows, pl.ds(256 * (unit - 8), 256)]
+
+    def ag(unit, kind, ref, peer):
+        return pltpu.make_async_remote_copy(
+            src_ref=ref,
+            dst_ref=ref,
+            send_sem=ag_send.at[unit, kind],
+            recv_sem=ag_recv.at[unit, kind],
+            device_id=peer,
+            device_id_type=MESH_ID,
+        )
+
+    def ag_out(unit, kind):
+        shard, part, peer = (
+            (fs, None, peer_core),
+            (fs, None, peer_x),
+            (fs, None, peer_y),
+            (fs_x, 0, peer_y),
+            (fs_y, 1, peer_x),
+            (fs_x, None, peer_core),
+            (fs_y, None, peer_core),
+            (fs_diag, 0, peer_core),
+            (fs_diag, 1, peer_core),
+        )[kind]
+        return ag(unit, kind, weight(unit, shard, part), peer)
+
+    def ag_in(unit, kind):
+        shard, part = (
+            (fs_core, None),
+            (fs_x, None),
+            (fs_y, None),
+            (fs_diag, 0),
+            (fs_diag, 1),
+            (fs_x + flip, None),
+            (fs_y + flip, None),
+            (fs_diag + flip, 0),
+            (fs_diag + flip, 1),
+        )[kind]
+        return ag(unit, kind, weight(unit, shard, part), peer_core)
+
+    def ag_own(unit):
+        if unit < N_AG:
+            for kind in (1, 2, 0):
+                ag_out(unit, kind).start()
+
+    def ag_relay(unit):
+        if 0 <= unit < N_AG:
+            ag_in(unit, 1).wait_recv()
+            ag_out(unit, 3).start()
+            ag_in(unit, 2).wait_recv()
+            ag_out(unit, 4).start()
+            ag_out(unit, 5).start()
+            ag_out(unit, 6).start()
+
+    def ag_last(unit):
+        if 0 <= unit < N_AG:
+            ag_in(unit, 3).wait_recv()
+            ag_out(unit, 7).start()
+            ag_in(unit, 4).wait_recv()
+            ag_out(unit, 8).start()
+
+    def pump(unit):
+        ag_relay(unit)
+        ag_last(unit - 1)
+        ag_own(unit + 3)
+
+    def ready(unit):
+        for kind in (0, 5, 6, 7, 8):
+            ag_in(unit, kind).wait_recv()
+
+    def side(index, src, dst, peer):
+        return pltpu.make_async_remote_copy(
+            src_ref=src,
+            dst_ref=dst,
+            send_sem=side_send.at[index],
+            recv_sem=side_recv.at[index],
+            device_id=peer,
+            device_id_type=MESH_ID,
+        )
+
+    chip_slot = fs - core
+    row_slot = 4 * yb
+
+    def param_copy(step, start, count, peer):
+        ref = small_in.at[pl.ds(start, count)]
+        return side(step, ref, ref, peer)
+
+    param_steps = (
+        (fs, 1, peer_core, fs_core),
+        (chip_slot, 2, peer_x, chip_slot + 2 - 4 * xb),
+        (row_slot, 4, peer_y, 4 - row_slot),
+    )
+
+    def param_start(step):
+        start, count, peer, _ = param_steps[step]
+        param_copy(step, start, count, peer).start()
+
+    def param_wait(step):
+        _, count, peer, land = param_steps[step]
+        param_copy(step, land, count, peer).wait_recv()
+
+    face_steps = (
+        (dp, 1, fs, 1, peer_core, dp, fs_core),
+        (dp, 1, chip_slot, 2, peer_x, dp, chip_slot + 2 - 4 * xb),
+        (dp, 1, row_slot, 4, peer_y, dp, 4 - row_slot),
+        (dp, 1, 0, 8, (fs, dp_pair), dp_pair, 0),
+        (2 * half_z, 2, 0, 8, (fs, dp_far), 2 - 2 * half_z, 0),
+    )
+
+    def face_copy(step, landing):
+        d0, dn, f0, fn, peer, ld, lf = face_steps[step]
+        if landing:
+            d0, f0 = ld, lf
+        ref = faces.at[span(64 * d0 + 8 * f0, 8 * dn * fn, 8), :]
+        return side(3 + step, ref, ref, peer)
+
+    def face_start(step):
+        face_copy(step, False).start()
+
+    def face_wait(step):
+        face_copy(step, True).wait_recv()
+
+    sum_peers = (peer_core, peer_x, peer_y, (fs, dp_pair), (fs, dp_far))
+
+    def sum_copy(step):
+        return side(8 + step, small_sum.at[step], small_land.at[step], sum_peers[step])
+
+    def sum_start(step):
+        sum_copy(step).start()
+
+    def sum_wait(step):
+        sum_copy(step).wait_recv()
+        small_sum[step + 1] = small_sum[step] + small_land[step]
+
+    def grad(unit, rows):
+        if unit == D_UNIT:
+            return sdn.at[rows, :]
+        if unit >= 4:
+            return act.at[rows, pl.ds(768 * (unit - 4), 768)]
+        return wts.at[4 + unit, rows, :]
+
+    def shape_of(unit):
+        return 384 if unit == D_UNIT else 96
+
+    def piece_shard(delta, which):
+        chip_x = (xb + delta % 2) - 2 * xb * (delta % 2)
+        chip_y = (yb + delta // 2) - 2 * yb * (delta // 2)
+        return (chip_y * 2 + chip_x) * 2 + which
+
+    def piece(unit, delta, which, part=None):
+        size = shape_of(unit)
+        shard = piece_shard(delta, which)
+        if part is None:
+            return grad(unit, span(size * shard, size))
+        return grad(unit, span(size * shard + (size // 2) * part, size // 2))
+
+    def lands(pair, unit, slot):
+        wide, down_only = pair
+        return down_only.at[slot] if unit == D_UNIT else wide.at[unit, slot]
+
+    def accumulate(dst, *sources):
+        rows = dst.shape[0]
+
+        def body(i, carry):
+            r = span(i * 48, 48)
+            value = dst[r, :].astype(F32)
+            for source in sources:
+                value = value + source[r, :].astype(F32)
+            dst[r, :] = value.astype(BF)
+            return carry
+
+        lax.fori_loop(0, rows // 48, body, 0)
+
+    def core_copy(unit, delta):
+        return pltpu.make_async_remote_copy(
+            src_ref=piece(unit, delta, 1 - core),
+            dst_ref=lands((lc, lcd), unit, delta),
+            send_sem=core_send.at[unit, delta],
+            recv_sem=core_recv.at[unit, delta],
+            device_id=peer_core,
+            device_id_type=MESH_ID,
+        )
+
+    def rs_core(unit):
+        for delta in (3, 2, 1, 0):
+            core_copy(unit, delta).start()
+
+    xy_kinds = (
+        (3, 0, (lx, lxd), 0, peer_x),
+        (3, 1, (ly, lyd), 0, peer_y),
+        (1, 0, (lx, lxd), 1, peer_x),
+        (2, 1, (ly, lyd), 1, peer_y),
+        (2, 0, (ly, lyd), 2, peer_y),
+        (1, 1, (lx, lxd), 2, peer_x),
+    )
+
+    def xy_copy(unit, kind):
+        delta, part, pair, slot, peer = xy_kinds[kind]
+        return pltpu.make_async_remote_copy(
+            src_ref=piece(unit, delta, core, part),
+            dst_ref=lands(pair, unit, slot),
+            send_sem=xy_send.at[unit, kind],
+            recv_sem=xy_recv.at[unit, kind],
+            device_id=peer,
+            device_id_type=MESH_ID,
+        )
+
+    def rs_first_piece(unit, delta):
+        core_copy(unit, delta).wait_recv()
+        accumulate(piece(unit, delta, core), lands((lc, lcd), unit, delta))
+        for kind in {3: (0, 1), 1: (2,), 2: (3,), 0: ()}[delta]:
+            xy_copy(unit, kind).start()
+
+    def rs_first(unit):
+        for delta in (3, 2, 1, 0):
+            rs_first_piece(unit, delta)
+
+    def rs_second(unit):
+        xy_copy(unit, 0).wait_recv()
+        accumulate(piece(unit, 2, core, 0), lands((lx, lxd), unit, 0))
+        xy_copy(unit, 4).start()
+        xy_copy(unit, 1).wait_recv()
+        accumulate(piece(unit, 1, core, 1), lands((ly, lyd), unit, 0))
+        xy_copy(unit, 5).start()
+
+    def z_copy(unit, index, src, slot, target):
+        return pltpu.make_async_remote_copy(
+            src_ref=src,
+            dst_ref=lands((lz, lzd), unit, slot),
+            send_sem=z_send.at[unit, index],
+            recv_sem=z_recv.at[unit, slot],
+            device_id=(fs, target),
+            device_id_type=MESH_ID,
+        )
+
+    def z_land(unit, slot):
+        return lands((lz, lzd), unit, slot)
+
+    def z_wait(unit, slot):
+        z_copy(unit, 0, z_land(unit, slot), slot, dp_pair).wait_recv()
+
+    def z_out(unit, index):
+        own_far = piece(unit, 0, core, far)
+        own_near = piece(unit, 0, core, near)
+        end = {
+            0: (own_far, 1, dp_inner),
+            1: (own_near, 0, dp_inner),
+        }
+        mid = {
+            0: (own_far, 2, dp_mid),
+            1: (z_land(unit, 2), 2, dp_end),
+            2: (z_land(unit, 2), 3, dp_mid),
+            3: (z_land(unit, 3), 3, dp_end),
+        }
+        return end.get(index), mid[index]
+
+    def z_end(unit, index):
+        return z_copy(unit, index, *z_out(unit, index)[0])
+
+    def z_mid(unit, index):
+        return z_copy(unit, index, *z_out(unit, index)[1])
+
+    def rs_own(unit):
+        for kind in (2, 3, 4, 5):
+            xy_copy(unit, kind).wait_recv()
+        accumulate(piece(unit, 0, core, 0), lands((lx, lxd), unit, 1), lands((ly, lyd), unit, 2))
+        accumulate(piece(unit, 0, core, 1), lands((ly, lyd), unit, 1), lands((lx, lxd), unit, 2))
+
+        @pl.when(is_end)
+        def _():
+            z_end(unit, 0).start()
+            z_end(unit, 1).start()
+
+    def rs_z2(unit):
+        @pl.when(is_mid)
+        def _():
+            z_wait(unit, 1)
+            accumulate(piece(unit, 0, core, far), z_land(unit, 1))
+            z_mid(unit, 0).start()
+
+    def rs_z3(unit):
+        @pl.when(is_mid)
+        def _():
+            z_wait(unit, 0)
+            z_wait(unit, 2)
+            accumulate(z_land(unit, 2), z_land(unit, 0), piece(unit, 0, core, near))
+            z_mid(unit, 1).start()
+            z_mid(unit, 2).start()
+
+    def rs_z4(unit):
+        @pl.when(is_mid)
+        def _():
+            z_wait(unit, 3)
+            z_mid(unit, 3).start()
+
+    def result_copy(unit, slot):
+        size = shape_of(unit) // 2
+        rows = span(size * (near if slot == 2 else far), size)
+        target = down_out.at[rows, :] if unit == D_UNIT else units_out.at[unit, rows, :]
+        return pltpu.make_async_copy(z_land(unit, slot), target, local_sem.at[16 + 2 * unit + slot - 2])
+
+    def rs_done(unit):
+        @pl.when(is_end)
+        def _():
+            z_wait(unit, 2)
+            z_wait(unit, 3)
+
+        for slot in (2, 3):
+            result_copy(unit, slot).start()
+
+    for copy in own_copies:
+        copy.wait()
+    small_copy.wait()
+    for unit in range(3):
+        ag_own(unit)
+    param_start(0)
+
+    img_h = gm
+    img_k = att
+    img_v = h1
+    img_gain = psmall_ref
+    zero_tail = jnp.zeros((16, 768), BF)
+
+    def image_norm(i):
+        values = patches_ref[i].astype(F32)
+        scaled, _ = norm_rows(values)
+        normed = scaled * img_gain[0:1, :] + img_gain[6:7, :]
+        img_h[span(64 * i + 48, 16), :] = zero_tail
+        img_h[span(64 * i, 50), :] = normed.astype(BF)
+        face_rows[0, pl.ds(i, 1), :] = values[0:1, :]
+        face_rows[1, pl.ds(i, 1), :] = normed[0:1, :]
+
+    loop(8, image_norm)
+    pqkv_copy.wait()
+
+    def image_kv(i):
+        r = span(i * TILE, TILE)
+        img_k[r, :] = nn(img_h[r, :], act[pl.ds(0, 768), pl.ds(768, 768)]).astype(BF)
+        img_v[r, :] = (nn(img_h[r, :], act[pl.ds(0, 768), pl.ds(1536, 768)]) + img_gain[3:4, :]).astype(BF)
+
+    loop(2, image_kv)
+    param_wait(0)
+    param_start(1)
+    pump(0)
+
+    lane_head = lax.broadcasted_iota(jnp.int32, (8, 768), 1) // 64
+    img_q = (nn(face_rows[1].astype(BF), act[pl.ds(0, 768), pl.ds(0, 768)]) + img_gain[2:3, :]) * 0.125
+    img_q = img_q.astype(BF).astype(F32)
+    stacked = jnp.concatenate([jnp.where(lane_head == h, img_q, 0.0) for h in range(12)], axis=0).astype(BF)
+    scores = nt(stacked, img_k[pl.ds(0, 512), :])
+    token = lax.broadcasted_iota(jnp.int32, (96, 512), 1)
+    image_of = lax.broadcasted_iota(jnp.int32, (96, 512), 0) % 8
+    scores = jnp.where((token // 64 == image_of) & (token % 64 < 50), scores, -1e30)
+    expd = jnp.exp(scores - jnp.max(scores, axis=-1, keepdims=True))
+    probs = (expd / jnp.sum(expd, axis=-1, keepdims=True)).astype(BF)
+    mixed = nn(probs, img_v[pl.ds(0, 512), :])
+    joined = jnp.zeros((8, 768), F32)
+    for h in range(12):
+        joined = joined + jnp.where(lane_head == h, mixed[8 * h : 8 * h + 8, :], 0.0)
+    param_wait(1)
+    param_start(2)
+    pump(1)
+    pout_copy.wait()
+    middle = face_rows[0] + (nn(joined.astype(BF), act[pl.ds(0, 768), pl.ds(2304, 768)]) + img_gain[4:5, :])
+    scaled, _ = norm_rows(middle)
+    normed = (scaled * img_gain[1:2, :] + img_gain[7:8, :]).astype(BF)
+    face_rows[0] = middle
+    pup_copy.wait()
+    for j in range(4):
+        hidden = nn(normed, dg[pl.ds(0, 768), pl.ds(768 * j, 768)]) + img_gain[8 + j : 9 + j, :]
+        face_rows[2 + j] = hidden * normal_cdf(hidden)
+    pump(2)
+    pdown_copy.wait()
+    total = face_rows[0] + img_gain[5:6, :]
+    for j in range(4):
+        total = total + nn(face_rows[2 + j].astype(BF), sdn[pl.ds(768 * j, 768), :])
+    unit_norm = total * lax.rsqrt(jnp.mean(total * total, axis=-1, keepdims=True) + 1e-06)
+    faces[span(64 * dp + 8 * fs, 8, 8), :] = unit_norm.astype(BF).astype(F32)
+    face_start(0)
+    param_wait(2)
+
+    flat_small = small_in[...].reshape(128, 128)
+    for r in range(4):
+        lane = lax.broadcasted_iota(jnp.int32, (128, 384), 0)
+        column = lax.broadcasted_iota(jnp.int32, (128, 384), 1)
+        pick = jnp.where((column == lane + 96 * r) & (lane < 96), 1.0, 0.0).astype(BF)
+        spread = nn(flat_small, pick)
+        for block in range(2):
+            shard = 4 * block + r
+            value = spread[16 * shard : 16 * shard + 8, :]
+            cols = slice(384 * block, 384 * block + 384)
+            if r == 0:
+                params[0:8, cols] = value
+            else:
+                params[0:8, cols] = params[0:8, cols] + value
+        for shard in range(8):
+            value = spread[16 * shard + 8 + r : 16 * shard + 9 + r, :]
+            row = 8 + shard // 2
+            cols = slice(384 * (shard % 2), 384 * (shard % 2) + 384)
+            if r == 0:
+                params[row : row + 1, cols] = value
+            else:
+                params[row : row + 1, cols] = params[row : row + 1, cols] + value
+
+    x_copy.wait()
+
+    def first_norm(i):
+        r = span(32 * i, 32)
+        scaled, _ = norm_rows(h2[r, :].astype(F32))
+        h1[r, :] = (scaled * params[0:1, :] + params[6:7, :]).astype(BF)
+
+    loop(32, first_norm)
+    for group in range(8):
+        same = lax.broadcasted_iota(jnp.int32, (64, 128), 0) == caprow_ref[group : group + 1, :]
+        member[:, 128 * group : 128 * group + 128] = jnp.where(same, 1.0, 0.0).astype(BF)
+    face_wait(0)
+    face_start(1)
+    pump(3)
+
+    def project(j):
+        def body(i):
+            r = span(TILE * i, TILE)
+            value = nn(h1[r, :], wts[j])
+            if j == 0:
+                value = (value + params[2:3, :]) * 0.125
+            if j == 2:
+                value = value + params[3:4, :]
+            qkv[r, pl.ds(768 * j, 768)] = value.astype(BF)
+
+        loop(4, body)
+
+    ready(0)
+    project(0)
+    ready(1)
+    project(1)
+    pump(4)
+    ready(2)
+    project(2)
+    face_wait(1)
+    face_start(2)
+
+    low_lane = lax.broadcasted_iota(jnp.int32, (128, 128), 1) < 64
+    zero_block = jnp.zeros((128, 128), BF)
+
+    def split_heads(block):
+        return jnp.concatenate(
+            [jnp.where(low_lane, block, zero_block), jnp.where(low_lane, zero_block, block)], axis=0
+        )
+
+    def join_heads(value):
+        return jnp.where(low_lane, value[0:128, :], value[128:256, :])
+
+    def same_caption(group):
+        part = member[:, span(128 * group, 128, 128)]
+        same = tn(part, part)
+        return jnp.concatenate([same, same], axis=0) > 0.5
+
+    def attention_probs(same, queries, keys):
+        value = jnp.where(same, nt(queries, keys), -1e30)
+        expd = jnp.exp(value - jnp.max(value, axis=-1, keepdims=True))
+        return expd * (1.0 / jnp.sum(expd, axis=-1, keepdims=True))
+
+    def attend(group):
+        r = span(128 * group, 128)
+        same = same_caption(group)
+        for hp in range(6):
+            queries = split_heads(qkv[r, pl.ds(128 * hp, 128)])
+            probs = attention_probs(same, queries, qkv[r, pl.ds(768 + 128 * hp, 128)])
+            mixed = nn(probs.astype(BF), qkv[r, pl.ds(1536 + 128 * hp, 128)])
+            att[r, pl.ds(128 * hp, 128)] = join_heads(mixed).astype(BF)
+
+    loop(8, attend, {1: [lambda: pump(5)], 4: [lambda: pump(6)], 7: [lambda: pump(7)]})
+    face_wait(2)
+    face_start(3)
+    ready(3)
+
+    def out_project(i):
+        r = span(TILE * i, TILE)
+        x1[r, :] = h2[r, :].astype(F32) + (nn(att[r, :], wts[3]) + params[4:5, :])
+
+    loop(4, out_project)
+
+    def second_norm(i):
+        r = span(32 * i, 32)
+        scaled, _ = norm_rows(x1[r, :])
+        h2[r, :] = (scaled * params[1:2, :] + params[7:8, :]).astype(BF)
+
+    loop(32, second_norm)
+    face_wait(3)
+    face_start(4)
+    pump(8)
+
+    def widen(j):
+        def body(i):
+            r = span(TILE * i, TILE)
+            work[...] = nn(h2[r, :], wts[4 + j]) + params[8 + j : 9 + j, :]
+
+            def gelu(k):
+                inner = span(16 * k, 16)
+                hidden = work[inner, :]
+                cdf = normal_cdf(hidden)
+                outer = span(TILE * i + 16 * k, 16)
+                act[outer, pl.ds(768 * j, 768)] = (hidden * cdf).astype(BF)
+                slope = cdf + hidden * (jnp.exp(-0.5 * hidden * hidden) * (1.0 / math.sqrt(2.0 * math.pi)))
+                dg[outer, pl.ds(768 * j, 768)] = slope.astype(BF)
+
+            loop(16, gelu)
+
+        loop(4, body)
+
+    for j in range(4):
+        ready(4 + j)
+        widen(j)
+        if j < 2:
+            pump(9 + j)
+        elif j == 2:
+            ag_last(10)
+    face_wait(4)
+
+    for jd in range(3):
+        ready(8 + jd)
+        cols = pl.ds(256 * jd, 256)
+
+        def narrow(i, cols=cols, jd=jd):
+            r = span(TILE * i, TILE)
+            value = nn(act[r, :], wdn[:, cols]) + params[5:6, 256 * jd : 256 * jd + 256]
+            value = x1[r, cols] + value
+            top = value.astype(BF)
+            rest = (value - top.astype(F32)).astype(BF)
+            lanes = span(TILE * i, TILE, 128)
+            piece_sum = nn(member[:, lanes], top) + nn(member[:, lanes], rest)
+
+            @pl.when(i == 0)
+            def _():
+                pooled[:, cols] = piece_sum
+
+            @pl.when(i > 0)
+            def _():
+                pooled[:, cols] = pooled[:, cols] + piece_sum
+
+        loop(4, narrow)
+
+    count = jnp.sum(member[...].astype(F32), axis=-1, keepdims=True)
+    mean_rows = pooled[...] / count
+    inverse = lax.rsqrt(jnp.mean(mean_rows * mean_rows, axis=-1, keepdims=True) + 1e-06)
+    embed = mean_rows * inverse
+    face_all = faces[...].astype(BF)
+    amount = sharp_ref[0] * (1.0 / math.sqrt(768.0))
+    match = amount * nt(embed.astype(BF), face_all) + offset_ref[0]
+    slot = lax.broadcasted_iota(jnp.int32, (64, 256), 1)
+    image_id = ((slot // 8) % 8) * 32 + (slot // 64) * 8 + slot % 8
+    positive = described_ref[...] == image_id
+    signed = jnp.where(positive, -match, match)
+    terms = jnp.maximum(signed, 0.0) + jnp.log1p(jnp.exp(-jnp.abs(signed)))
+    row_loss = jnp.sum(terms, axis=-1, keepdims=True) * (1.0 / 256.0)
+    loss_out[...] = jnp.broadcast_to(row_loss, (64, 128))
+    slope = ((jax.nn.sigmoid(match) - jnp.where(positive, 1.0, 0.0)) * amount).astype(BF)
+    grad_embed = nn(slope, face_all)
+    grad_pooled = inverse * (grad_embed - embed * jnp.mean(grad_embed * embed, axis=-1, keepdims=True))
+    per_caption = grad_pooled / count
+    caption_hi[...] = per_caption.astype(BF)
+    caption_lo[...] = (per_caption - caption_hi[...].astype(F32)).astype(BF)
+
+    def spread_down(i):
+        gm[span(TILE * i, TILE), :] = tn(member[:, span(TILE * i, TILE, 128)], caption_hi[...]).astype(BF)
+
+    loop(4, spread_down)
+
+    for unit in range(N_AG):
+        for kind in range(9):
+            ag_out(unit, kind).wait_send()
+    for step in range(3):
+        start, sent, peer, _ = param_steps[step]
+        param_copy(step, start, sent, peer).wait_send()
+    for step in range(5):
+        face_copy(step, False).wait_send()
+
+    ones = jnp.ones((16, 1024), BF)
+
+    def column_sum(value):
+        return nn(ones, value)[0:1, :]
+
+    def down_piece(delta):
+        def body(i):
+            which = (1 - core) + i * (2 * core - 1)
+            shard = piece_shard(delta, which)
+            sdn[span(384 * shard, 384), :] = tn(act[:, span(384 * shard, 384, 128)], gm[...]).astype(BF)
+
+            @pl.when(i == 0)
+            def _():
+                core_copy(D_UNIT, delta).start()
+
+        loop(2, body)
+
+    down_piece(3)
+    down_piece(2)
+    rs_first_piece(D_UNIT, 3)
+    down_piece(1)
+    rs_first_piece(D_UNIT, 2)
+    down_piece(0)
+    rs_first_piece(D_UNIT, 1)
+    rs_first_piece(D_UNIT, 0)
+
+    def hidden_back(i):
+        r = span(TILE * i, TILE)
+        for jj in range(3):
+            cols = pl.ds(1024 * jj, 1024)
+            value = nt(gm[r, :], wdn[pl.ds(1024 * jj, 1024), :])
+            dg[r, cols] = (dg[r, cols].astype(F32) * value).astype(BF)
+
+    loop(4, hidden_back, {1: [lambda: rs_second(D_UNIT)]})
+    partial_rows = {}
+
+    def up_unit(j):
+        def body(i):
+            act[span(TILE * i, TILE), pl.ds(768 * j, 768)] = tn(
+                h2[:, span(TILE * i, TILE, 128)], dg[:, pl.ds(768 * j, 768)]
+            ).astype(BF)
+
+        loop(3, body)
+        rs_core(4 + j)
+        small_sum[0, 8 + j : 9 + j, :] = column_sum(dg[:, pl.ds(768 * j, 768)])
+
+    up_unit(0)
+    up_unit(1)
+    rs_first(4)
+    up_unit(2)
+    rs_first(5)
+    up_unit(3)
+    rs_first(6)
+    rs_own(D_UNIT)
+    small_sum[0, 5:6, :] = column_sum(gm[...])
+    partial[...] = jnp.zeros((4, 8, 768), F32)
+
+    def fold(value):
+        return value.reshape(value.shape[0] // 8, 8, 768).sum(axis=0)
+
+    def middle_back(i):
+        r = span(TILE * i, TILE)
+        total = nt(dg[r, pl.ds(0, 768)], wts[4])
+        for j in range(1, 4):
+            total = total + nt(dg[r, pl.ds(768 * j, 768)], wts[4 + j])
+        work[...] = total
+        faces[...] = tn(member[:, span(TILE * i, TILE, 128)], caption_lo[...])
+
+        def rows_back(k):
+            inner = span(16 * k, 16)
+            outer = span(TILE * i + 16 * k, 16)
+            upstream = work[inner, :]
+            scaled, inverse = norm_rows(x1[outer, :])
+            partial[0] = partial[0] + fold(upstream * scaled)
+            partial[1] = partial[1] + fold(upstream)
+            weighted = upstream * params[1:2, :]
+            first_mean = jnp.mean(weighted, axis=-1, keepdims=True)
+            second_mean = jnp.mean(weighted * scaled, axis=-1, keepdims=True)
+            value = gm[outer, :].astype(F32) + faces[inner, :]
+            value = value + inverse * (weighted - first_mean - scaled * second_mean)
+            x1[outer, :] = value
+            gm[outer, :] = value.astype(BF)
+
+        loop(16, rows_back)
+
+    loop(
+        4,
+        middle_back,
+        {
+            0: [lambda: rs_first(7)],
+            1: [lambda: rs_second(4)],
+            2: [lambda: rs_z2(D_UNIT)],
+            3: [lambda: rs_second(5)],
+        },
+    )
+    x_again = pltpu.make_async_copy(x_hbm, h2, local_sem.at[15])
+    x_again.start()
+
+    def out_unit(i):
+        wts[7, span(TILE * i, TILE), :] = tn(att[:, span(TILE * i, TILE, 128)], gm[...]).astype(BF)
+
+    loop(3, out_unit)
+    rs_core(3)
+    small_sum[0, 4:5, :] = column_sum(gm[...])
+
+    def attended_back(i):
+        r = span(TILE * i, TILE)
+        att[r, :] = nt(gm[r, :], wts[3]).astype(BF)
+
+    loop(4, attended_back)
+    rs_second(6)
+    rs_first(3)
+    rs_own(4)
+    rs_z3(D_UNIT)
+
+    def attend_back(group):
+        r = span(128 * group, 128)
+        same = same_caption(group)
+        for hp in range(6):
+            qs = pl.ds(128 * hp, 128)
+            ks = pl.ds(768 + 128 * hp, 128)
+            vs = pl.ds(1536 + 128 * hp, 128)
+            queries = split_heads(qkv[r, qs])
+            keys = qkv[r, ks]
+            upstream = split_heads(att[r, qs])
+            probs = attention_probs(same, queries, keys)
+            probs_grad = nt(upstream, qkv[r, vs])
+            inner = jnp.sum(probs * probs_grad, axis=-1, keepdims=True)
+            score_grad = (probs * (probs_grad - inner)).astype(BF)
+            qkv[r, vs] = tn(probs.astype(BF), upstream).astype(BF)
+            qkv[r, ks] = tn(score_grad, queries).astype(BF)
+            qkv[r, qs] = (join_heads(nn(score_grad, keys)).astype(BF).astype(F32) * 0.125).astype(BF)
+
+    loop(
+        8,
+        attend_back,
+        {
+            1: [lambda: rs_z2(4), lambda: rs_own(5), lambda: rs_second(7)],
+            3: [lambda: rs_z2(5), lambda: rs_z3(4), lambda: rs_own(6), lambda: rs_second(3)],
+            5: [lambda: rs_z4(D_UNIT), lambda: rs_z2(6), lambda: rs_z3(5), lambda: rs_own(7)],
+            7: [lambda: rs_z2(7), lambda: rs_z3(6), lambda: rs_z4(4), lambda: rs_own(3)],
+        },
+    )
+
+    def qkv_unit(j):
+        def body(i):
+            wts[4 + j, span(TILE * i, TILE), :] = tn(
+                h1[:, span(TILE * i, TILE, 128)], qkv[:, pl.ds(768 * j, 768)]
+            ).astype(BF)
+
+        loop(3, body)
+        rs_core(j)
+
+    qkv_unit(0)
+    rs_z2(3)
+    rs_z3(7)
+    rs_z4(5)
+    qkv_unit(1)
+    rs_first(0)
+    rs_z3(3)
+    rs_z4(6)
+    qkv_unit(2)
+    rs_first(1)
+    rs_z4(7)
+    small_sum[0, 2:3, :] = column_sum(qkv[:, pl.ds(0, 768)])
+    small_sum[0, 3:4, :] = column_sum(qkv[:, pl.ds(1536, 768)])
+    x_again.wait()
+
+    def input_back(i):
+        r = span(TILE * i, TILE)
+        total = nt(qkv[r, pl.ds(0, 768)], wts[0])
+        for j in range(1, 3):
+            total = total + nt(qkv[r, pl.ds(768 * j, 768)], wts[j])
+        work[...] = total
+
+        def rows_back(k):
+            inner = span(16 * k, 16)
+            outer = span(TILE * i + 16 * k, 16)
+            upstream = work[inner, :]
+            scaled, inverse = norm_rows(h2[outer, :].astype(F32))
+            partial[2] = partial[2] + fold(upstream * scaled)
+            partial[3] = partial[3] + fold(upstream)
+            weighted = upstream * params[0:1, :]
+            first_mean = jnp.mean(weighted, axis=-1, keepdims=True)
+            second_mean = jnp.mean(weighted * scaled, axis=-1, keepdims=True)
+            value = x1[outer, :] + inverse * (weighted - first_mean - scaled * second_mean)
+            att[outer, :] = value.astype(BF)
+
+        loop(16, rows_back)
+
+    loop(
+        4,
+        input_back,
+        {
+            0: [lambda: rs_first(2), lambda: rs_second(0)],
+            1: [lambda: rs_second(1), lambda: rs_z4(3)],
+            2: [lambda: rs_own(0)],
+            3: [lambda: rs_second(2), lambda: rs_z2(0), lambda: rs_own(1)],
+        },
+    )
+    input_copy = pltpu.make_async_copy(att, input_out, local_sem.at[34])
+    input_copy.start()
+    for row, index in ((0, 2), (1, 0), (6, 3), (7, 1)):
+        small_sum[0, row : row + 1, :] = jnp.sum(partial[index], axis=0, keepdims=True)
+    small_sum[0, 12:16, :] = jnp.zeros((4, 768), F32)
+    sum_start(0)
+    rs_z3(0)
+    rs_z2(1)
+    sum_wait(0)
+    sum_start(1)
+    for unit in (D_UNIT, 4, 5, 6, 7, 3):
+        rs_done(unit)
+    rs_own(2)
+    sum_wait(1)
+    sum_start(2)
+    rs_z4(0)
+    rs_z3(1)
+    rs_z2(2)
+    sum_wait(2)
+    sum_start(3)
+    rs_z4(1)
+    rs_done(0)
+    rs_z3(2)
+    sum_wait(3)
+    sum_start(4)
+    rs_done(1)
+    rs_z4(2)
+    sum_wait(4)
+    small_out[...] = small_sum[5]
+    rs_done(2)
+
+    input_copy.wait()
+    for unit in range(9):
+        for slot in (2, 3):
+            result_copy(unit, slot).wait()
+        for delta in range(4):
+            core_copy(unit, delta).wait_send()
+        for kind in range(6):
+            xy_copy(unit, kind).wait_send()
+
+        @pl.when(is_end)
+        def _(unit=unit):
+            for index in range(2):
+                z_end(unit, index).wait_send()
+
+        @pl.when(is_mid)
+        def _(unit=unit):
+            for index in range(4):
+                z_mid(unit, index).wait_send()
+
+    for step in range(5):
+        sum_copy(step).wait_send()
+
+
+def fused_step(
+    incoming_word_states,
+    sentence_number_per_word,
+    described_picture,
+    lookup_matrices,
+    mixer_exit_matrix,
+    widening_matrix,
+    narrowing_matrix,
+    normalizer_multipliers,
+    word_offsets,
+    widened_offset,
+    picture_patches,
+    picture_lookup_matrices,
+    picture_mixer_exit_matrix,
+    picture_widening_matrix,
+    picture_narrowing_matrix,
+    picture_normalizer_multipliers,
+    picture_offsets,
+    picture_widened_offset,
+    sharpness_coefficient,
+    objective_offset,
+):
+    rows, length, width = incoming_word_states.shape
+    tokens = rows * length
+    small = jnp.concatenate(
+        [normalizer_multipliers, word_offsets, widened_offset.reshape(4, 96)], axis=0
+    )
+    small = jnp.pad(small, ((0, 4), (0, 32)))
+    picture_small = jnp.concatenate(
+        [picture_normalizer_multipliers, picture_offsets, picture_widened_offset.reshape(4, width)], axis=0
+    )
+    picture_small = jnp.pad(picture_small.astype(F32), ((0, 4), (0, 0)))
+    caption = sentence_number_per_word + CAPS * jnp.arange(rows, dtype=jnp.int32)[:, None]
+    vmem = pl.BlockSpec(memory_space=pltpu.VMEM)
+    hbm = pl.BlockSpec(memory_space=pl.ANY)
+    smem = pl.BlockSpec(memory_space=pltpu.SMEM)
+    dma = pltpu.SemaphoreType.DMA
+    outs = pl.pallas_call(
+        fused_kernel,
+        out_shape=(
+            jax.ShapeDtypeStruct((8, 96, width), BF),
+            jax.ShapeDtypeStruct((384, width), BF),
+            jax.ShapeDtypeStruct((tokens, width), BF),
+            jax.ShapeDtypeStruct((16, width), F32),
+            jax.ShapeDtypeStruct((64, 128), F32),
+        ),
+        in_specs=[smem, smem, hbm, vmem, vmem, hbm, hbm, hbm, hbm, hbm, vmem, hbm, hbm, hbm, hbm, vmem],
+        out_specs=(hbm, hbm, hbm, vmem, vmem),
+        scratch_shapes=[
+            pltpu.VMEM((8, 768, 768), BF),
+            pltpu.VMEM((3072, 768), BF),
+            pltpu.VMEM((1024, 768), BF),
+            pltpu.VMEM((1024, 2304), BF),
+            pltpu.VMEM((1024, 768), BF),
+            pltpu.VMEM((1024, 768), F32),
+            pltpu.VMEM((1024, 768), BF),
+            pltpu.VMEM((1024, 3072), BF),
+            pltpu.VMEM((1024, 3072), BF),
+            pltpu.VMEM((1024, 768), BF),
+            pltpu.VMEM((3072, 768), BF),
+            pltpu.VMEM((8, 4, 96, 768), BF),
+            pltpu.VMEM((4, 384, 768), BF),
+            pltpu.VMEM((8, 3, 48, 768), BF),
+            pltpu.VMEM((3, 192, 768), BF),
+            pltpu.VMEM((8, 3, 48, 768), BF),
+            pltpu.VMEM((3, 192, 768), BF),
+            pltpu.VMEM((8, 4, 48, 768), BF),
+            pltpu.VMEM((4, 192, 768), BF),
+            pltpu.VMEM((TILE, 768), F32),
+            pltpu.VMEM((TILE, 768), F32),
+            pltpu.VMEM((8, 16, 128), BF),
+            pltpu.VMEM((16, 768), F32),
+            pltpu.VMEM((64, 1024), BF),
+            pltpu.VMEM((64, 768), F32),
+            pltpu.VMEM((64, 768), BF),
+            pltpu.VMEM((64, 768), BF),
+            pltpu.VMEM((4, 8, 768), F32),
+            pltpu.VMEM((6, 16, 768), F32),
+            pltpu.VMEM((5, 16, 768), F32),
+            pltpu.VMEM((6, 8, 768), F32),
+            dma((N_AG, 9)),
+            dma((N_AG, 9)),
+            dma((9, 4)),
+            dma((9, 4)),
+            dma((9, 6)),
+            dma((9, 6)),
+            dma((9, 4)),
+            dma((9, 4)),
+            dma((13,)),
+            dma((13,)),
+            dma((35,)),
+        ],
+        compiler_params=pltpu.CompilerParams(
+            collective_id=0, has_side_effects=True, vmem_limit_bytes=67043328
+        ),
+        name="lit_step",
+    )(
+        sharpness_coefficient,
+        objective_offset,
+        incoming_word_states.reshape(tokens, width),
+        caption.reshape(tokens // 128, 128),
+        described_picture.reshape(-1, 1),
+        lookup_matrices,
+        mixer_exit_matrix,
+        widening_matrix,
+        narrowing_matrix,
+        small,
+        picture_patches,
+        picture_lookup_matrices,
+        picture_mixer_exit_matrix,
+        picture_widening_matrix,
+        picture_narrowing_matrix,
+        picture_small,
+    )
+    units, down_part, input_part, small_part, loss_part = outs
+    place = lax.axis_index("fsdp")
+    columns = lax.dynamic_slice_in_dim(small_part[:8], place * 96, 96, axis=1)
+    hidden_part = lax.dynamic_slice_in_dim(small_part[8:12].reshape(-1), place * 384, 384)
+    wide = units.astype(F32)
+    return (
+        jnp.concatenate([wide[0], wide[1], wide[2]], axis=1),
+        wide[3],
+        jnp.concatenate([wide[4], wide[5], wide[6], wide[7]], axis=1),
+        down_part.astype(F32),
+        columns[:2],
+        columns[2:8],
+        hidden_part,
+        input_part.reshape(rows, length, width),
+        loss_part[:, 0],
+    )
+
+
 def solution(mesh):
+    fits = mesh.shape["fsdp"] == 8 and mesh.shape["dp"] == 4
     return jax.shard_map(
-        per_device,
+        fused_step if fits else per_device,
         mesh=mesh,
         in_specs=(
             P(("fsdp", "dp"), None, None),

time: 633 us -> 251 us (0.40); the launches traced: 625 us -> 250 us
  Pallas kernels: 0 us -> 227 us
  waiting for transfers between devices: 176 us -> 0 us
  matrix products: 171 us -> 0 us
  blocking collectives: 140 us -> 0 us
  local copies, waits for them, and re-layouts: 83.4 us -> 13.4 us
  other arithmetic: 37.2 us -> 8.06 us
  between operations: 16.3 us -> 1.98 us
    pallas_call x0 -> x1, Pallas kernels: none -> 227 us  [fused_step(): pl.pallas_call(fused_kernel, out_shape=(jax.ShapeDtypeStruct((8, 96, widt...]
    dot_general x28 -> x0, matrix products: 171 us -> none  [the longest x1 38.3 us: forward_block(): jnp.dot(second_low, up_w, preferred_element_type=jnp.float32)]
    reduce_scatter x4 -> x0, waiting for transfers between devices: 153 us -> none  [per_device(): lax.psum_scatter(piece_grad.astype(jnp.bfloat16), 'fsdp', scatter_dimensi...]
    all_gather x4 -> x0, blocking collectives: 98.6 us -> none  [the longest x1 73.4 us: per_device(): piece = lax.all_gather(image_embed, ('fsdp', 'dp'), axis=0, tiled=True)]
    reshape x17 -> x5, local copies, waits for them, and re-layouts: 48 us -> 3.5 us  [the longest x1 1.36 us: fused_step(): described_picture.reshape(-1, 1)]
    psum x1 -> x0, blocking collectives: 41.4 us -> none  [per_device(): small = lax.psum(small, ('fsdp', 'dp'))]
    convert_element_type x17 -> x2, other arithmetic: 24 us -> 2.56 us  [the longest x1 1.47 us: fused_step(): wide = units.astype(F32)]
    psum x1 -> x0, waiting for transfers between devices: 20.9 us -> none  [per_device(): lax.psum(lax.psum_scatter(piece_grad.astype(jnp.bfloat16), 'fsdp', scatte...]
  transfers between devices with their start and end apart: 9 -> 0, of which waited for: 4 -> 0; matrix products, arithmetic and copies ran while one was open for 30% -> 0% of each run, Pallas kernels for 0% -> 0%
where the time goes in v2:
time: 251 us; the launch traced here: 250 us
  Pallas kernels  227 us (90%)
  local copies, waits for them, and re-layouts  13.4 us (5%)
  other arithmetic  8.06 us (3%)
    pallas_call x1, Pallas kernels, fused_step(): pl.pallas_call(fused_kernel, out_shape=(jax.ShapeDtypeStruct((8, 96, widt...  227 us

profile of v2, /device:TPU:0, one launch (start us, length us, event | category | flops | bytes accessed | tf_op | source)
XLA Modules:
  0.0 250.4 jit_solution(17156130592333671625)
XLA Ops:
  1.9 0.8 reshape.47
  2.7 1.3 fusion.14.small_hbm
  4.0 0.7 reshape.48
  4.7 0.8 broadcast_add_fusion
  5.5 0.7 reshape.45.caprow_ref
  6.1 1.4 copy.31.described_ref
  7.5 1.3 fusion.5.psmall_ref
  8.8 2.0 copy.32.patches_ref
  10.9 227.0 %lit_step.1 = (bf16[8,96,768]{2,1,0:T(8,128)(2,1)}, bf16[384,768]{1,0:T(8,128)(2,1)}, bf16[1024,768]{1,0:T(8,128)(2,1)}, f32[16,768]{1,0:T(8,128)}, f32[64,128]{1,0:T(8,128)}) custom-call(f32[1]{0:T(128)S(6)} %copy.34.sharp_ref, f32[1]{0:T(128)S(6)} %copy.35.offset_ref, bf16[1024,768]{1,0:T(8,128)(2,1)} %bitcast.19, s32[8,128]{1,0:T(8,128)} %reshape.45.caprow_ref, ...), custom_call_target="tpu_custom_call" | custom-call | tf_op jit(solution)/shard_map/lit_step/pallas_call | solution.py:1362
  237.8 1.4 slice_reduce_fusion
  239.2 0.7 slice.50
  240.0 0.7 slice.47
  240.7 0.1 constant_dynamic-slice_fusion
  240.8 0.7 dynamic_slice.7
  241.4 0.6 slice.48
  242.0 0.6 slice.49
  242.6 1.5 convert_element_type.11
  244.1 0.9 slice_bitcast_fusion.3
  244.9 1.1 pad_maximum_fusion
  246.1 0.0 copy-start.1
  246.1 1.0 pad_maximum_fusion.1
  247.0 0.4 copy-done.1
  247.4 0.0 copy-start
  247.4 1.1 convert_element_type.12
  248.5 0.7 copy-done
  249.2 1.1 copy.36
  (2 shorter events, 0.0 us)
Async XLA Ops:
  246.1 1.3 copy-start.1
  247.4 1.8 copy-start

commit v3 on v2

--- a/solution.py
+++ b/solution.py
@@ -323,6 +323,8 @@
 F32 = jnp.float32
 MESH_ID = pl.DeviceIdType.MESH
 TILE = 256
+ROWS = 128
+GROUPS = 2
 N_AG = 11
 D_UNIT = 8
 
@@ -374,19 +376,23 @@
     sharp_ref,
     offset_ref,
     x_hbm,
-    caprow_ref,
+    segment_ref,
     described_ref,
     qkv_hbm,
     out_hbm,
     up_hbm,
     down_hbm,
-    small_hbm,
-    patches_ref,
+    gain_ref,
+    shift_ref,
+    hidden_ref,
+    patches_hbm,
     pqkv_hbm,
     pout_hbm,
     pup_hbm,
     pdown_hbm,
-    psmall_ref,
+    pgain_ref,
+    pshift_ref,
+    phidden_ref,
     units_out,
     down_out,
     input_out,
@@ -415,6 +421,7 @@
     faces,
     small_in,
     params,
+    img_gain,
     member,
     pooled,
     caption_hi,
@@ -477,13 +484,17 @@
     own_copies.append(fetch(out_hbm, wts.at[3, own_rows, :]))
     own_copies += [fetch(up_hbm.at[:, pl.ds(768 * j, 768)], wts.at[4 + j, own_rows, :]) for j in range(4)]
     own_copies.append(fetch(down_hbm, wdn.at[span(384 * fs, 384), :]))
-    small_copy = fetch(small_hbm, small_in.at[fs])
+    patches_copy = fetch(patches_hbm, gm.at[pl.ds(512, 400), :])
     pqkv_copy = fetch(pqkv_hbm, act.at[pl.ds(0, 768), pl.ds(0, 2304)])
     x_copy = fetch(x_hbm, h2)
     pout_copy = fetch(pout_hbm, act.at[pl.ds(0, 768), pl.ds(2304, 768)])
     pup_copy = fetch(pup_hbm, dg.at[pl.ds(0, 768), :])
     pdown_copy = fetch(pdown_hbm, sdn)
 
+    small_in[fs] = jnp.zeros((16, 128), F32)
+    small_in[fs, 0:2, 0:96] = gain_ref[...].astype(F32)
+    small_in[fs, 2:8, 0:96] = shift_ref[...].astype(F32)
+    small_in[fs, 8:11, :] = hidden_ref[...].astype(F32)
     pl.semaphore_wait(barrier, len(greet))
 
     def weight(unit, shard, part=None):
@@ -493,9 +504,18 @@
         rows = span(384 * shard, 384) if part is None else span(384 * shard + 192 * part, 192)
         return wdn.at[rows, pl.ds(256 * (unit - 8), 256)]
 
-    def ag(unit, kind, ref, peer):
+    def own_weight(unit):
+        if unit < 3:
+            return qkv_hbm.at[:, pl.ds(768 * unit, 768)]
+        if unit == 3:
+            return out_hbm
+        if unit < 8:
+            return up_hbm.at[:, pl.ds(768 * (unit - 4), 768)]
+        return down_hbm.at[:, pl.ds(256 * (unit - 8), 256)]
+
+    def ag(unit, kind, ref, peer, source=None):
         return pltpu.make_async_remote_copy(
-            src_ref=ref,
+            src_ref=ref if source is None else source,
             dst_ref=ref,
             send_sem=ag_send.at[unit, kind],
             recv_sem=ag_recv.at[unit, kind],
@@ -515,7 +535,7 @@
             (fs_diag, 0, peer_core),
             (fs_diag, 1, peer_core),
         )[kind]
-        return ag(unit, kind, weight(unit, shard, part), peer)
+        return ag(unit, kind, weight(unit, shard, part), peer, own_weight(unit) if kind < 3 else None)
 
     def ag_in(unit, kind):
         shard, part = (
@@ -801,9 +821,6 @@
         for slot in (2, 3):
             result_copy(unit, slot).start()
 
-    for copy in own_copies:
-        copy.wait()
-    small_copy.wait()
     for unit in range(3):
         ag_own(unit)
     param_start(0)
@@ -811,19 +828,25 @@
     img_h = gm
     img_k = att
     img_v = h1
-    img_gain = psmall_ref
-    zero_tail = jnp.zeros((16, 768), BF)
+    img_gain[0:2, :] = pgain_ref[...].astype(F32)
+    img_gain[2:8, :] = pshift_ref[...].astype(F32)
+    phidden = phidden_ref[...].astype(F32)
+    for q in range(24):
+        img_gain[8 + q // 6 : 9 + q // 6, 128 * (q % 6) : 128 * (q % 6) + 128] = phidden[q : q + 1, :]
+    img_h[pl.ds(400, 112), :] = jnp.zeros((112, 768), BF)
+    patches_copy.wait()
+
+    def image_normed(values):
+        return norm_rows(values)[0] * img_gain[0:1, :] + img_gain[6:7, :]
+
+    first_rows = img_h[pl.ds(512, 16), :].astype(F32)[0:8, :]
+    face_rows[0] = first_rows
+    face_rows[1] = image_normed(first_rows)
 
     def image_norm(i):
-        values = patches_ref[i].astype(F32)
-        scaled, _ = norm_rows(values)
-        normed = scaled * img_gain[0:1, :] + img_gain[6:7, :]
-        img_h[span(64 * i + 48, 16), :] = zero_tail
-        img_h[span(64 * i, 50), :] = normed.astype(BF)
-        face_rows[0, pl.ds(i, 1), :] = values[0:1, :]
-        face_rows[1, pl.ds(i, 1), :] = normed[0:1, :]
-
-    loop(8, image_norm)
+        img_h[span(80 * i, 80), :] = image_normed(img_h[span(512 + 80 * i, 80), :].astype(F32)).astype(BF)
+
+    loop(5, image_norm)
     pqkv_copy.wait()
 
     def image_kv(i):
@@ -843,7 +866,7 @@
     scores = nt(stacked, img_k[pl.ds(0, 512), :])
     token = lax.broadcasted_iota(jnp.int32, (96, 512), 1)
     image_of = lax.broadcasted_iota(jnp.int32, (96, 512), 0) % 8
-    scores = jnp.where((token // 64 == image_of) & (token % 64 < 50), scores, -1e30)
+    scores = jnp.where((token % 8 == image_of) & (token < 400), scores, -1e30)
     expd = jnp.exp(scores - jnp.max(scores, axis=-1, keepdims=True))
     probs = (expd / jnp.sum(expd, axis=-1, keepdims=True)).astype(BF)
     mixed = nn(probs, img_v[pl.ds(0, 512), :])
@@ -872,7 +895,7 @@
     face_start(0)
     param_wait(2)
 
-    flat_small = small_in[...].reshape(128, 128)
+    flat_small = small_in[...].reshape(128, 128).astype(BF)
     for r in range(4):
         lane = lax.broadcasted_iota(jnp.int32, (128, 384), 0)
         column = lax.broadcasted_iota(jnp.int32, (128, 384), 1)
@@ -886,16 +909,14 @@
                 params[0:8, cols] = value
             else:
                 params[0:8, cols] = params[0:8, cols] + value
-        for shard in range(8):
-            value = spread[16 * shard + 8 + r : 16 * shard + 9 + r, :]
-            row = 8 + shard // 2
-            cols = slice(384 * (shard % 2), 384 * (shard % 2) + 384)
-            if r == 0:
-                params[row : row + 1, cols] = value
-            else:
-                params[row : row + 1, cols] = params[row : row + 1, cols] + value
+    for shard in range(8):
+        for q in range(3):
+            at = 384 * (shard % 2) + 128 * q
+            params[8 + shard // 2 : 9 + shard // 2, at : at + 128] = small_in[shard, 8 + q : 9 + q, :]
 
     x_copy.wait()
+    for copy in own_copies:
+        copy.wait()
 
     def first_norm(i):
         r = span(32 * i, 32)
@@ -904,7 +925,8 @@
 
     loop(32, first_norm)
     for group in range(8):
-        same = lax.broadcasted_iota(jnp.int32, (64, 128), 0) == caprow_ref[group : group + 1, :]
+        rows = [segment_ref[2 * group + k : 2 * group + k + 1, :] + CAPS * (2 * group + k) for k in range(2)]
+        same = lax.broadcasted_iota(jnp.int32, (64, 128), 0) == jnp.concatenate(rows, axis=1)
         member[:, 128 * group : 128 * group + 128] = jnp.where(same, 1.0, 0.0).astype(BF)
     face_wait(0)
     face_start(1)
@@ -1042,11 +1064,13 @@
     match = amount * nt(embed.astype(BF), face_all) + offset_ref[0]
     slot = lax.broadcasted_iota(jnp.int32, (64, 256), 1)
     image_id = ((slot // 8) % 8) * 32 + (slot // 64) * 8 + slot % 8
-    positive = described_ref[...] == image_id
+    diagonal = lax.broadcasted_iota(jnp.int32, (64, 64), 0) == lax.broadcasted_iota(jnp.int32, (64, 64), 1)
+    described = jnp.where(diagonal, described_ref[...].astype(F32), 0.0)
+    positive = jnp.sum(described, axis=-1, keepdims=True) == image_id.astype(F32)
     signed = jnp.where(positive, -match, match)
     terms = jnp.maximum(signed, 0.0) + jnp.log1p(jnp.exp(-jnp.abs(signed)))
     row_loss = jnp.sum(terms, axis=-1, keepdims=True) * (1.0 / 256.0)
-    loss_out[...] = jnp.broadcast_to(row_loss, (64, 128))
+    loss_out[...] = jnp.sum(jnp.where(diagonal, row_loss, 0.0), axis=0, keepdims=True)
     slope = ((jax.nn.sigmoid(match) - jnp.where(positive, 1.0, 0.0)) * amount).astype(BF)
     grad_embed = nn(slope, face_all)
     grad_pooled = inverse * (grad_embed - embed * jnp.mean(grad_embed * embed, axis=-1, keepdims=True))
@@ -1137,8 +1161,8 @@
         faces[...] = tn(member[:, span(TILE * i, TILE, 128)], caption_lo[...])
 
         def rows_back(k):
-            inner = span(16 * k, 16)
-            outer = span(TILE * i + 16 * k, 16)
+            inner = span(ROWS * k, ROWS)
+            outer = span(TILE * i + ROWS * k, ROWS)
             upstream = work[inner, :]
             scaled, inverse = norm_rows(x1[outer, :])
             partial[0] = partial[0] + fold(upstream * scaled)
@@ -1151,7 +1175,7 @@
             x1[outer, :] = value
             gm[outer, :] = value.astype(BF)
 
-        loop(16, rows_back)
+        loop(TILE // ROWS, rows_back)
 
     loop(
         4,
@@ -1183,69 +1207,92 @@
     rs_own(4)
     rs_z3(D_UNIT)
 
-    def attend_back(group):
-        r = span(128 * group, 128)
-        same = same_caption(group)
-        for hp in range(6):
-            qs = pl.ds(128 * hp, 128)
-            ks = pl.ds(768 + 128 * hp, 128)
-            vs = pl.ds(1536 + 128 * hp, 128)
+    def attend_back(quad):
+        def chain(group, same, half):
+            r = span(128 * group, 128)
+            at = 256 * quad + 128 * half
+            qs = pl.ds(at, 128)
             queries = split_heads(qkv[r, qs])
-            keys = qkv[r, ks]
+            keys = qkv[r, pl.ds(768 + at, 128)]
             upstream = split_heads(att[r, qs])
             probs = attention_probs(same, queries, keys)
-            probs_grad = nt(upstream, qkv[r, vs])
+            probs_grad = nt(upstream, qkv[r, pl.ds(1536 + at, 128)])
             inner = jnp.sum(probs * probs_grad, axis=-1, keepdims=True)
             score_grad = (probs * (probs_grad - inner)).astype(BF)
-            qkv[r, vs] = tn(probs.astype(BF), upstream).astype(BF)
-            qkv[r, ks] = tn(score_grad, queries).astype(BF)
-            qkv[r, qs] = (join_heads(nn(score_grad, keys)).astype(BF).astype(F32) * 0.125).astype(BF)
+            to = 768 * quad + 128 * half
+            dg[r, pl.ds(to + 512, 128)] = tn(probs.astype(BF), upstream).astype(BF)
+            dg[r, pl.ds(to + 256, 128)] = tn(score_grad, queries).astype(BF)
+            query_grad = join_heads(nn(score_grad, keys)).astype(BF).astype(F32)
+            dg[r, pl.ds(to, 128)] = (query_grad * 0.125).astype(BF)
+
+        def body(i):
+            for group in range(GROUPS):
+                same = same_caption(GROUPS * i + group)
+                for half in range(2):
+                    chain(GROUPS * i + group, same, half)
+
+        return body
+
+    def qkv_unit(quad):
+        def body(i):
+            wts[4 + quad, span(TILE * i, TILE), :] = tn(
+                h1[:, span(TILE * i, TILE, 128)], dg[:, pl.ds(768 * quad, 768)]
+            ).astype(BF)
+
+        loop(3, body)
+        rs_core(quad)
 
     loop(
-        8,
-        attend_back,
+        8 // GROUPS,
+        attend_back(0),
         {
             1: [lambda: rs_z2(4), lambda: rs_own(5), lambda: rs_second(7)],
             3: [lambda: rs_z2(5), lambda: rs_z3(4), lambda: rs_own(6), lambda: rs_second(3)],
-            5: [lambda: rs_z4(D_UNIT), lambda: rs_z2(6), lambda: rs_z3(5), lambda: rs_own(7)],
-            7: [lambda: rs_z2(7), lambda: rs_z3(6), lambda: rs_z4(4), lambda: rs_own(3)],
         },
     )
-
-    def qkv_unit(j):
-        def body(i):
-            wts[4 + j, span(TILE * i, TILE), :] = tn(
-                h1[:, span(TILE * i, TILE, 128)], qkv[:, pl.ds(768 * j, 768)]
-            ).astype(BF)
-
-        loop(3, body)
-        rs_core(j)
-
     qkv_unit(0)
-    rs_z2(3)
-    rs_z3(7)
-    rs_z4(5)
+    loop(
+        8 // GROUPS,
+        attend_back(1),
+        {
+            0: [lambda: rs_first(0)],
+            1: [lambda: rs_z4(D_UNIT), lambda: rs_z2(6), lambda: rs_z3(5), lambda: rs_own(7)],
+            3: [lambda: rs_second(0), lambda: rs_z2(7), lambda: rs_z3(6), lambda: rs_z4(4), lambda: rs_own(3)],
+        },
+    )
     qkv_unit(1)
-    rs_first(0)
-    rs_z3(3)
-    rs_z4(6)
+    loop(
+        8 // GROUPS,
+        attend_back(2),
+        {
+            0: [lambda: rs_first(1), lambda: rs_z2(3)],
+            1: [lambda: rs_own(0), lambda: rs_z3(7), lambda: rs_z4(5)],
+            3: [lambda: rs_second(1), lambda: rs_z2(0), lambda: rs_z3(3), lambda: rs_z4(6)],
+        },
+    )
     qkv_unit(2)
-    rs_first(1)
+    rs_own(1)
+    rs_z3(0)
     rs_z4(7)
-    small_sum[0, 2:3, :] = column_sum(qkv[:, pl.ds(0, 768)])
-    small_sum[0, 3:4, :] = column_sum(qkv[:, pl.ds(1536, 768)])
+    rs_first(2)
+    for quad in range(3):
+        to = slice(256 * quad, 256 * quad + 256)
+        small_sum[0, 2:3, to] = column_sum(dg[:, pl.ds(768 * quad, 256)])
+        small_sum[0, 3:4, to] = column_sum(dg[:, pl.ds(768 * quad + 512, 256)])
     x_again.wait()
 
     def input_back(i):
         r = span(TILE * i, TILE)
-        total = nt(qkv[r, pl.ds(0, 768)], wts[0])
-        for j in range(1, 3):
-            total = total + nt(qkv[r, pl.ds(768 * j, 768)], wts[j])
+        total = jnp.zeros((TILE, 768), F32)
+        for quad in range(3):
+            for j in range(3):
+                part = dg[r, pl.ds(768 * quad + 256 * j, 256)]
+                total = total + nt(part, wts[j, :, pl.ds(256 * quad, 256)])
         work[...] = total
 
         def rows_back(k):
-            inner = span(16 * k, 16)
-            outer = span(TILE * i + 16 * k, 16)
+            inner = span(ROWS * k, ROWS)
+            outer = span(TILE * i + ROWS * k, ROWS)
             upstream = work[inner, :]
             scaled, inverse = norm_rows(h2[outer, :].astype(F32))
             partial[2] = partial[2] + fold(upstream * scaled)
@@ -1256,16 +1303,16 @@
             value = x1[outer, :] + inverse * (weighted - first_mean - scaled * second_mean)
             att[outer, :] = value.astype(BF)
 
-        loop(16, rows_back)
+        loop(TILE // ROWS, rows_back)
 
     loop(
         4,
         input_back,
         {
-            0: [lambda: rs_first(2), lambda: rs_second(0)],
-            1: [lambda: rs_second(1), lambda: rs_z4(3)],
-            2: [lambda: rs_own(0)],
-            3: [lambda: rs_second(2), lambda: rs_z2(0), lambda: rs_own(1)],
+            0: [lambda: rs_second(2), lambda: rs_z2(1), lambda: rs_z4(3)],
+            1: [lambda: rs_own(2), lambda: rs_z4(0)],
+            2: [lambda: rs_z3(1)],
+            3: [lambda: rs_z2(2)],
         },
     )
     input_copy = pltpu.make_async_copy(att, input_out, local_sem.at[34])
@@ -1274,30 +1321,23 @@
         small_sum[0, row : row + 1, :] = jnp.sum(partial[index], axis=0, keepdims=True)
     small_sum[0, 12:16, :] = jnp.zeros((4, 768), F32)
     sum_start(0)
-    rs_z3(0)
-    rs_z2(1)
+    rs_z4(1)
+    rs_z3(2)
     sum_wait(0)
     sum_start(1)
-    for unit in (D_UNIT, 4, 5, 6, 7, 3):
+    for unit in (D_UNIT, 4, 5, 6, 7, 3, 0):
         rs_done(unit)
-    rs_own(2)
     sum_wait(1)
     sum_start(2)
-    rs_z4(0)
-    rs_z3(1)
-    rs_z2(2)
+    rs_z4(2)
     sum_wait(2)
     sum_start(3)
-    rs_z4(1)
-    rs_done(0)
-    rs_z3(2)
+    rs_done(1)
     sum_wait(3)
     sum_start(4)
-    rs_done(1)
-    rs_z4(2)
+    rs_done(2)
     sum_wait(4)
     small_out[...] = small_sum[5]
-    rs_done(2)
 
     input_copy.wait()
     for unit in range(9):
@@ -1320,6 +1360,71 @@
 
     for step in range(5):
         sum_copy(step).wait_send()
+
+
+def finish_kernel(
+    units_hbm,
+    down_hbm,
+    input_hbm,
+    small_ref,
+    loss_ref,
+    qkv_out,
+    out_out,
+    up_out,
+    down_out,
+    gain_out,
+    shift_out,
+    hidden_out,
+    input_out,
+    loss_out,
+    units,
+    down,
+    tokens,
+    qkv,
+    out,
+    up,
+    down_wide,
+    sem,
+):
+    fs = lax.axis_index("fsdp")
+
+    def move(src, dst, index):
+        copy = pltpu.make_async_copy(src, dst, sem.at[index])
+        copy.start()
+        return copy
+
+    units_in = move(units_hbm, units, 0)
+    down_in = move(down_hbm, down, 1)
+    tokens_in = move(input_hbm, tokens, 2)
+    for shard in range(8):
+
+        @pl.when(fs == shard)
+        def _(shard=shard):
+            gain_out[...] = small_ref[0:2, 96 * shard : 96 * shard + 96]
+            shift_out[...] = small_ref[2:8, 96 * shard : 96 * shard + 96]
+            for q in range(3):
+                at = 384 * (shard % 2) + 128 * q
+                hidden_out[q : q + 1, :] = small_ref[8 + shard // 2 : 9 + shard // 2, at : at + 128]
+
+    loss_out[...] = loss_ref[...]
+    units_in.wait()
+    for quad in range(3):
+        for j in range(3):
+            at = 768 * j + 256 * quad
+            qkv[:, at : at + 256] = units[quad, :, 256 * j : 256 * j + 256].astype(F32)
+    moves = [move(qkv, qkv_out, 3)]
+    out[...] = units[3].astype(F32)
+    moves.append(move(out, out_out, 4))
+    for j in range(4):
+        up[:, 768 * j : 768 * j + 768] = units[4 + j].astype(F32)
+    moves.append(move(up, up_out, 5))
+    down_in.wait()
+    down_wide[...] = down[...].astype(F32)
+    moves.append(move(down_wide, down_out, 6))
+    tokens_in.wait()
+    moves.append(move(tokens, input_out, 7))
+    for copy in moves:
+        copy.wait()
 
 
 def fused_step(
@@ -1346,15 +1451,6 @@
 ):
     rows, length, width = incoming_word_states.shape
     tokens = rows * length
-    small = jnp.concatenate(
-        [normalizer_multipliers, word_offsets, widened_offset.reshape(4, 96)], axis=0
-    )
-    small = jnp.pad(small, ((0, 4), (0, 32)))
-    picture_small = jnp.concatenate(
-        [picture_normalizer_multipliers, picture_offsets, picture_widened_offset.reshape(4, width)], axis=0
-    )
-    picture_small = jnp.pad(picture_small.astype(F32), ((0, 4), (0, 0)))
-    caption = sentence_number_per_word + CAPS * jnp.arange(rows, dtype=jnp.int32)[:, None]
     vmem = pl.BlockSpec(memory_space=pltpu.VMEM)
     hbm = pl.BlockSpec(memory_space=pl.ANY)
     smem = pl.BlockSpec(memory_space=pltpu.SMEM)
@@ -1366,9 +1462,9 @@
             jax.ShapeDtypeStruct((384, width), BF),
             jax.ShapeDtypeStruct((tokens, width), BF),
             jax.ShapeDtypeStruct((16, width), F32),
-            jax.ShapeDtypeStruct((64, 128), F32),
+            jax.ShapeDtypeStruct((1, 64), F32),
         ),
-        in_specs=[smem, smem, hbm, vmem, vmem, hbm, hbm, hbm, hbm, hbm, vmem, hbm, hbm, hbm, hbm, vmem],
+        in_specs=[smem, smem, hbm, vmem, vmem, *[hbm] * 4, *[vmem] * 3, *[hbm] * 5, *[vmem] * 3],
         out_specs=(hbm, hbm, hbm, vmem, vmem),
         scratch_shapes=[
             pltpu.VMEM((8, 768, 768), BF),
@@ -1392,7 +1488,8 @@
             pltpu.VMEM((4, 192, 768), BF),
             pltpu.VMEM((TILE, 768), F32),
             pltpu.VMEM((TILE, 768), F32),
-            pltpu.VMEM((8, 16, 128), BF),
+            pltpu.VMEM((8, 16, 128), F32),
+            pltpu.VMEM((16, 768), F32),
             pltpu.VMEM((16, 768), F32),
             pltpu.VMEM((64, 1024), BF),
             pltpu.VMEM((64, 768), F32),
@@ -1422,36 +1519,57 @@
         sharpness_coefficient,
         objective_offset,
         incoming_word_states.reshape(tokens, width),
-        caption.reshape(tokens // 128, 128),
-        described_picture.reshape(-1, 1),
+        sentence_number_per_word,
+        described_picture.reshape(1, -1),
         lookup_matrices,
         mixer_exit_matrix,
         widening_matrix,
         narrowing_matrix,
-        small,
-        picture_patches,
+        normalizer_multipliers,
+        word_offsets,
+        widened_offset.reshape(3, 128),
+        picture_patches.transpose(1, 0, 2).reshape(-1, width),
         picture_lookup_matrices,
         picture_mixer_exit_matrix,
         picture_widening_matrix,
         picture_narrowing_matrix,
-        picture_small,
-    )
-    units, down_part, input_part, small_part, loss_part = outs
-    place = lax.axis_index("fsdp")
-    columns = lax.dynamic_slice_in_dim(small_part[:8], place * 96, 96, axis=1)
-    hidden_part = lax.dynamic_slice_in_dim(small_part[8:12].reshape(-1), place * 384, 384)
-    wide = units.astype(F32)
-    return (
-        jnp.concatenate([wide[0], wide[1], wide[2]], axis=1),
-        wide[3],
-        jnp.concatenate([wide[4], wide[5], wide[6], wide[7]], axis=1),
-        down_part.astype(F32),
-        columns[:2],
-        columns[2:8],
-        hidden_part,
-        input_part.reshape(rows, length, width),
-        loss_part[:, 0],
-    )
+        picture_normalizer_multipliers,
+        picture_offsets,
+        picture_widened_offset.reshape(24, 128),
+    )
+    finished = pl.pallas_call(
+        finish_kernel,
+        out_shape=(
+            jax.ShapeDtypeStruct((96, 2304), F32),
+            jax.ShapeDtypeStruct((96, width), F32),
+            jax.ShapeDtypeStruct((96, 3072), F32),
+            jax.ShapeDtypeStruct((384, width), F32),
+            jax.ShapeDtypeStruct((2, 96), F32),
+            jax.ShapeDtypeStruct((6, 96), F32),
+            jax.ShapeDtypeStruct((3, 128), F32),
+            jax.ShapeDtypeStruct((tokens, width), BF),
+            jax.ShapeDtypeStruct((1, 64), F32),
+        ),
+        in_specs=[hbm, hbm, hbm, vmem, vmem],
+        out_specs=(hbm, hbm, hbm, hbm, vmem, vmem, vmem, hbm, vmem),
+        scratch_shapes=[
+            pltpu.VMEM((8, 96, width), BF),
+            pltpu.VMEM((384, width), BF),
+            pltpu.VMEM((tokens, width), BF),
+            pltpu.VMEM((96, 2304), F32),
+            pltpu.VMEM((96, width), F32),
+            pltpu.VMEM((96, 3072), F32),
+            pltpu.VMEM((384, width), F32),
+            dma((8,)),
+        ],
+        compiler_params=pltpu.CompilerParams(vmem_limit_bytes=60 * 2**20),
+        name="lit_finish",
+    )(*outs)
+    finished = list(finished)
+    finished[6] = finished[6].reshape(-1)
+    finished[7] = finished[7].reshape(rows, length, width)
+    finished[8] = finished[8].reshape(-1)
+    return tuple(finished)
 
 
 def solution(mesh):

time: 251 us -> 205 us (0.82)
  Pallas kernels: 227 us -> 202 us
  local copies, waits for them, and re-layouts: 13.4 us -> 0 us
  other arithmetic: 8.06 us -> 0 us
    pallas_call x1, Pallas kernels: 227 us -> 197 us  [fused_step(): pl.pallas_call(fused_kernel, out_shape=(jax.ShapeDtypeStruct((8, 96, widt...]
    pallas_call x0 -> x1, Pallas kernels: none -> 5.1 us  [fused_step(): pl.pallas_call(finish_kernel, out_shape=(jax.ShapeDtypeStruct((96, 2304),...]
    unnamed x6 -> x0, local copies, waits for them, and re-layouts: 4.27 us -> none
    slice x5 -> x0, local copies, waits for them, and re-layouts: 4.02 us -> none  [the longest x1 1.38 us: fused_step(): loss_part[:, 0]]
    reshape x5 -> x0, local copies, waits for them, and re-layouts: 3.5 us -> none  [the longest x1 1.36 us: fused_step(): described_picture.reshape(-1, 1)]
    concatenate x3 -> x0, other arithmetic: 3.38 us -> none  [the longest x1 1.29 us: fused_step(): jnp.concatenate([normalizer_multipliers, word_offsets, widened_offset.res...]
    convert_element_type x2 -> x0, other arithmetic: 2.56 us -> none  [the longest x1 1.47 us: fused_step(): wide = units.astype(F32)]
where the time goes in v3:
time: 205 us; the launch traced here: 204 us
  Pallas kernels  202 us (99%)
  between operations  2.13 us (1%)
    pallas_call x1, Pallas kernels, fused_step(): pl.pallas_call(fused_kernel, out_shape=(jax.ShapeDtypeStruct((8, 96, widt...  197 us
    pallas_call x1, Pallas kernels, fused_step(): pl.pallas_call(finish_kernel, out_shape=(jax.ShapeDtypeStruct((96, 2304),...  5.1 us

profile of v3, /device:TPU:0, one launch (start us, length us, event | category | flops | bytes accessed | tf_op | source)
XLA Modules:
  0.0 204.2 jit_solution(959680727920964756)
XLA Ops:
  1.9 196.9 %lit_step.1 = (bf16[8,96,768]{2,1,0:T(8,128)(2,1)}, bf16[384,768]{1,0:T(8,128)(2,1)}, bf16[1024,768]{1,0:T(8,128)(2,1)}, f32[16,768]{1,0:T(8,128)}, f32[1,64]{1,0:T(1,128)}) custom-call(f32[1]{0:T(128)S(6)} %copy.29.sharp_ref, f32[1]{0:T(128)S(6)} %copy.30.offset_ref, bf16[1024,768]{1,0:T(8,128)(2,1)} %bitcast.10, s32[16,64]{1,0:T(8,128)} %segment_ref.1, ...), custom_call_target="tpu_custom_call" | custom-call | tf_op jit(solution)/shard_map/lit_step/pallas_call | solution.py:1458
  198.9 5.1 %lit_finish.1 = (f32[96,2304]{1,0:T(8,128)}, f32[96,768]{1,0:T(8,128)}, f32[96,3072]{1,0:T(8,128)}, f32[384,768]{1,0:T(8,128)}, f32[2,96]{1,0:T(2,128)}, /*index...) custom-call(bf16[8,96,768]{2,1,0:T(8,128)(2,1)} %get-tuple-element.23.units_hbm, ...), custom_call_target="tpu_custom_call" | custom-call | tf_op jit(solution)/shard_map/lit_finish/pallas_call | solution.py:1540

commit v4 on v3

--- a/solution.py
+++ b/solution.py
@@ -326,6 +326,25 @@
 ROWS = 128
 GROUPS = 2
 N_AG = 11
+Z_PAIRS = ((0, 1), (3, 4), (6, 7), (9, 10))
+GATHER = {
+    "start": ("o0", "o1", "o7", "o3",),
+    "keys": ("r0", "r1", "o2",),
+    "mixed": ("l0", "r3", "o4",),
+    "image": ("l1", "o6", "r7", "z0", "r2", "l3", "o5",),
+    "norm": ("y0", "r4", "l2",),
+    "project1": ("o10", "r5", "r6",),
+    "project2": ("o9", "l4",),
+    "attend2": ("o8",),
+    "attend4": ("l6", "l7", "z1",),
+    "attend6": ("y1",),
+    "attend7": ("l5",),
+    "out": ("r9", "r10", "z2",),
+    "norm2": ("r8", "y2",),
+    "widen1": ("l8", "l10", "l9",),
+    "widen2": ("z3",),
+    "widen3": ("y3",),
+}
 D_UNIT = 8
 
 
@@ -418,6 +437,7 @@
     lz,
     lzd,
     work,
+    low,
     faces,
     small_in,
     params,
@@ -467,7 +487,8 @@
     dp_far = dp + 2 - 4 * half_z
 
     barrier = pltpu.get_barrier_semaphore()
-    greet = [peer_core, peer_x, peer_y, (fs, dp_pair), (fs, dp_far)]
+    others = (fs_core, fs_x, fs_y, fs_diag, fs_x + flip, fs_y + flip, fs_diag + flip)
+    greet = [(other, dp) for other in others] + [(fs, dp_pair), (fs, dp_far)]
     for peer in greet:
         pl.semaphore_signal(barrier, inc=1, device_id=peer, device_id_type=MESH_ID)
 
@@ -534,6 +555,10 @@
             (fs_y, None, peer_core),
             (fs_diag, 0, peer_core),
             (fs_diag, 1, peer_core),
+            (fs_x, None, (fs, dp_pair)),
+            (fs_y, None, (fs, dp_pair)),
+            (fs_diag, 0, (fs, dp_pair)),
+            (fs_diag, 1, (fs, dp_pair)),
         )[kind]
         return ag(unit, kind, weight(unit, shard, part), peer, own_weight(unit) if kind < 3 else None)
 
@@ -548,34 +573,97 @@
             (fs_y + flip, None),
             (fs_diag + flip, 0),
             (fs_diag + flip, 1),
+            (fs_x, None),
+            (fs_y, None),
+            (fs_diag, 0),
+            (fs_diag, 1),
         )[kind]
         return ag(unit, kind, weight(unit, shard, part), peer_core)
 
-    def ag_own(unit):
-        if unit < N_AG:
-            for kind in (1, 2, 0):
-                ag_out(unit, kind).start()
-
-    def ag_relay(unit):
-        if 0 <= unit < N_AG:
-            ag_in(unit, 1).wait_recv()
-            ag_out(unit, 3).start()
-            ag_in(unit, 2).wait_recv()
-            ag_out(unit, 4).start()
-            ag_out(unit, 5).start()
-            ag_out(unit, 6).start()
-
-    def ag_last(unit):
-        if 0 <= unit < N_AG:
-            ag_in(unit, 3).wait_recv()
-            ag_out(unit, 7).start()
-            ag_in(unit, 4).wait_recv()
-            ag_out(unit, 8).start()
-
-    def pump(unit):
-        ag_relay(unit)
-        ag_last(unit - 1)
-        ag_own(unit + 3)
+    def fetching(unit, body):
+        for pair in Z_PAIRS:
+            if unit in pair:
+                pl.when(dp % 2 == pair.index(unit))(body)
+                return
+        body()
+
+    def ag_own(*units):
+        for unit in units:
+
+            def body(unit=unit):
+                for kind in (1, 2):
+                    ag_out(unit, kind).start()
+
+            fetching(unit, body)
+            ag_out(unit, 0).start()
+
+    def handed(unit):
+        return any(unit in pair for pair in Z_PAIRS)
+
+    def ag_relay(*units):
+        for unit in units:
+
+            def body(unit=unit):
+                for arrived, onward, inner, across in ((1, 3, 5, 9), (2, 4, 6, 10)):
+                    ag_in(unit, arrived).wait_recv()
+                    ag_out(unit, onward).start()
+                    ag_out(unit, inner).start()
+                    if handed(unit):
+                        ag_out(unit, across).start()
+
+            fetching(unit, body)
+
+    def ag_last(*units):
+        for unit in units:
+
+            def body(unit=unit):
+                for arrived, inner, across in ((3, 7, 11), (4, 8, 12)):
+                    ag_in(unit, arrived).wait_recv()
+                    ag_out(unit, inner).start()
+                    if handed(unit):
+                        ag_out(unit, across).start()
+
+            fetching(unit, body)
+
+    def ag_across(pair, kinds):
+        for index in range(2):
+
+            @pl.when(dp % 2 != index)
+            def _(unit=pair[index]):
+                for arrived, inner in kinds:
+                    ag_in(unit, arrived).wait_recv()
+                    ag_out(unit, inner).start()
+
+    def z_relay(pair):
+        ag_across(pair, ((9, 5), (10, 6)))
+
+    def z_last(pair):
+        ag_across(pair, ((11, 7), (12, 8)))
+
+    def ag_drain():
+        for unit in range(N_AG):
+
+            def body(unit=unit):
+                for kind in (1, 2, 3, 4) + ((9, 10, 11, 12) if handed(unit) else ()):
+                    ag_out(unit, kind).wait_send()
+
+            fetching(unit, body)
+            for kind in (0, 5, 6, 7, 8):
+                ag_out(unit, kind).wait_send()
+
+    def hook(point):
+        for step in GATHER.get(point, ()):
+            number = int(step[1:])
+            if step[0] == "o":
+                ag_own(number)
+            elif step[0] == "r":
+                ag_relay(number)
+            elif step[0] == "l":
+                ag_last(number)
+            elif step[0] == "z":
+                z_relay(Z_PAIRS[number])
+            else:
+                z_last(Z_PAIRS[number])
 
     def ready(unit):
         for kind in (0, 5, 6, 7, 8):
@@ -594,38 +682,27 @@
     chip_slot = fs - core
     row_slot = 4 * yb
 
-    def param_copy(step, start, count, peer):
-        ref = small_in.at[pl.ds(start, count)]
-        return side(step, ref, ref, peer)
-
-    param_steps = (
-        (fs, 1, peer_core, fs_core),
-        (chip_slot, 2, peer_x, chip_slot + 2 - 4 * xb),
-        (row_slot, 4, peer_y, 4 - row_slot),
-    )
-
-    def param_start(step):
-        start, count, peer, _ = param_steps[step]
-        param_copy(step, start, count, peer).start()
-
-    def param_wait(step):
-        _, count, peer, land = param_steps[step]
-        param_copy(step, land, count, peer).wait_recv()
-
+    def param_copy(index, slot):
+        ref = small_in.at[slot]
+        return side(index, ref, ref, (others[index], dp))
+
+    far_plane = 2 - 2 * half_z
     face_steps = (
         (dp, 1, fs, 1, peer_core, dp, fs_core),
         (dp, 1, chip_slot, 2, peer_x, dp, chip_slot + 2 - 4 * xb),
         (dp, 1, row_slot, 4, peer_y, dp, 4 - row_slot),
-        (dp, 1, 0, 8, (fs, dp_pair), dp_pair, 0),
-        (2 * half_z, 2, 0, 8, (fs, dp_far), 2 - 2 * half_z, 0),
+        (dp, 1, 4 * core, 4, (fs, dp_pair), dp_pair, 4 * core),
+        (2 * half_z, 2, 4 * core, 4, (fs, dp_far), far_plane, 4 * core),
+        (dp_pair, 1, 4 * core, 4, peer_core, dp_pair, 4 - 4 * core),
+        (far_plane, 2, 4 * core, 4, peer_core, far_plane, 4 - 4 * core),
     )
 
     def face_copy(step, landing):
         d0, dn, f0, fn, peer, ld, lf = face_steps[step]
         if landing:
             d0, f0 = ld, lf
-        ref = faces.at[span(64 * d0 + 8 * f0, 8 * dn * fn, 8), :]
-        return side(3 + step, ref, ref, peer)
+        ref = faces.at[pl.ds(d0, dn), pl.ds(f0, fn)]
+        return side(7 + step, ref, ref, peer)
 
     def face_start(step):
         face_copy(step, False).start()
@@ -636,7 +713,7 @@
     sum_peers = (peer_core, peer_x, peer_y, (fs, dp_pair), (fs, dp_far))
 
     def sum_copy(step):
-        return side(8 + step, small_sum.at[step], small_land.at[step], sum_peers[step])
+        return side(14 + step, small_sum.at[step], small_land.at[step], sum_peers[step])
 
     def sum_start(step):
         sum_copy(step).start()
@@ -821,9 +898,9 @@
         for slot in (2, 3):
             result_copy(unit, slot).start()
 
-    for unit in range(3):
-        ag_own(unit)
-    param_start(0)
+    for index in range(7):
+        param_copy(index, fs).start()
+    hook("start")
 
     img_h = gm
     img_k = att
@@ -855,9 +932,7 @@
         img_v[r, :] = (nn(img_h[r, :], act[pl.ds(0, 768), pl.ds(1536, 768)]) + img_gain[3:4, :]).astype(BF)
 
     loop(2, image_kv)
-    param_wait(0)
-    param_start(1)
-    pump(0)
+    hook("keys")
 
     lane_head = lax.broadcasted_iota(jnp.int32, (8, 768), 1) // 64
     img_q = (nn(face_rows[1].astype(BF), act[pl.ds(0, 768), pl.ds(0, 768)]) + img_gain[2:3, :]) * 0.125
@@ -873,9 +948,7 @@
     joined = jnp.zeros((8, 768), F32)
     for h in range(12):
         joined = joined + jnp.where(lane_head == h, mixed[8 * h : 8 * h + 8, :], 0.0)
-    param_wait(1)
-    param_start(2)
-    pump(1)
+    hook("mixed")
     pout_copy.wait()
     middle = face_rows[0] + (nn(joined.astype(BF), act[pl.ds(0, 768), pl.ds(2304, 768)]) + img_gain[4:5, :])
     scaled, _ = norm_rows(middle)
@@ -885,15 +958,16 @@
     for j in range(4):
         hidden = nn(normed, dg[pl.ds(0, 768), pl.ds(768 * j, 768)]) + img_gain[8 + j : 9 + j, :]
         face_rows[2 + j] = hidden * normal_cdf(hidden)
-    pump(2)
+    hook("image")
     pdown_copy.wait()
     total = face_rows[0] + img_gain[5:6, :]
     for j in range(4):
         total = total + nn(face_rows[2 + j].astype(BF), sdn[pl.ds(768 * j, 768), :])
     unit_norm = total * lax.rsqrt(jnp.mean(total * total, axis=-1, keepdims=True) + 1e-06)
-    faces[span(64 * dp + 8 * fs, 8, 8), :] = unit_norm.astype(BF).astype(F32)
+    faces[dp, fs] = unit_norm.astype(BF)
     face_start(0)
-    param_wait(2)
+    for index in range(7):
+        param_copy(index, others[index]).wait_recv()
 
     flat_small = small_in[...].reshape(128, 128).astype(BF)
     for r in range(4):
@@ -930,7 +1004,7 @@
         member[:, 128 * group : 128 * group + 128] = jnp.where(same, 1.0, 0.0).astype(BF)
     face_wait(0)
     face_start(1)
-    pump(3)
+    hook("norm")
 
     def project(j):
         def body(i):
@@ -946,9 +1020,10 @@
 
     ready(0)
     project(0)
+    hook("project0")
     ready(1)
     project(1)
-    pump(4)
+    hook("project1")
     ready(2)
     project(2)
     face_wait(1)
@@ -984,7 +1059,8 @@
             mixed = nn(probs.astype(BF), qkv[r, pl.ds(1536 + 128 * hp, 128)])
             att[r, pl.ds(128 * hp, 128)] = join_heads(mixed).astype(BF)
 
-    loop(8, attend, {1: [lambda: pump(5)], 4: [lambda: pump(6)], 7: [lambda: pump(7)]})
+    hook("project2")
+    loop(8, attend, {i: [lambda i=i: hook(f"attend{i}")] for i in range(8)})
     face_wait(2)
     face_start(3)
     ready(3)
@@ -994,6 +1070,7 @@
         x1[r, :] = h2[r, :].astype(F32) + (nn(att[r, :], wts[3]) + params[4:5, :])
 
     loop(4, out_project)
+    hook("out")
 
     def second_norm(i):
         r = span(32 * i, 32)
@@ -1001,9 +1078,10 @@
         h2[r, :] = (scaled * params[1:2, :] + params[7:8, :]).astype(BF)
 
     loop(32, second_norm)
+    hook("norm2")
     face_wait(3)
     face_start(4)
-    pump(8)
+    face_start(5)
 
     def widen(j):
         def body(i):
@@ -1026,11 +1104,9 @@
     for j in range(4):
         ready(4 + j)
         widen(j)
-        if j < 2:
-            pump(9 + j)
-        elif j == 2:
-            ag_last(10)
+        hook(f"widen{j}")
     face_wait(4)
+    face_start(6)
 
     for jd in range(3):
         ready(8 + jd)
@@ -1055,11 +1131,14 @@
 
         loop(4, narrow)
 
+    face_wait(5)
+    face_wait(6)
+
     count = jnp.sum(member[...].astype(F32), axis=-1, keepdims=True)
     mean_rows = pooled[...] / count
     inverse = lax.rsqrt(jnp.mean(mean_rows * mean_rows, axis=-1, keepdims=True) + 1e-06)
     embed = mean_rows * inverse
-    face_all = faces[...].astype(BF)
+    face_all = faces[...].astype(F32).reshape(256, 768).astype(BF)
     amount = sharp_ref[0] * (1.0 / math.sqrt(768.0))
     match = amount * nt(embed.astype(BF), face_all) + offset_ref[0]
     slot = lax.broadcasted_iota(jnp.int32, (64, 256), 1)
@@ -1083,13 +1162,10 @@
 
     loop(4, spread_down)
 
-    for unit in range(N_AG):
-        for kind in range(9):
-            ag_out(unit, kind).wait_send()
-    for step in range(3):
-        start, sent, peer, _ = param_steps[step]
-        param_copy(step, start, sent, peer).wait_send()
-    for step in range(5):
+    ag_drain()
+    for index in range(7):
+        param_copy(index, fs).wait_send()
+    for step in range(7):
         face_copy(step, False).wait_send()
 
     ones = jnp.ones((16, 1024), BF)
@@ -1158,7 +1234,7 @@
         for j in range(1, 4):
             total = total + nt(dg[r, pl.ds(768 * j, 768)], wts[4 + j])
         work[...] = total
-        faces[...] = tn(member[:, span(TILE * i, TILE, 128)], caption_lo[...])
+        low[...] = tn(member[:, span(TILE * i, TILE, 128)], caption_lo[...]).astype(BF)
 
         def rows_back(k):
             inner = span(ROWS * k, ROWS)
@@ -1170,7 +1246,7 @@
             weighted = upstream * params[1:2, :]
             first_mean = jnp.mean(weighted, axis=-1, keepdims=True)
             second_mean = jnp.mean(weighted * scaled, axis=-1, keepdims=True)
-            value = gm[outer, :].astype(F32) + faces[inner, :]
+            value = gm[outer, :].astype(F32) + low[inner, :].astype(F32)
             value = value + inverse * (weighted - first_mean - scaled * second_mean)
             x1[outer, :] = value
             gm[outer, :] = value.astype(BF)
@@ -1487,7 +1563,8 @@
             pltpu.VMEM((8, 4, 48, 768), BF),
             pltpu.VMEM((4, 192, 768), BF),
             pltpu.VMEM((TILE, 768), F32),
-            pltpu.VMEM((TILE, 768), F32),
+            pltpu.VMEM((TILE, 768), BF),
+            pltpu.VMEM((4, 8, 8, 768), BF),
             pltpu.VMEM((8, 16, 128), F32),
             pltpu.VMEM((16, 768), F32),
             pltpu.VMEM((16, 768), F32),
@@ -1499,16 +1576,16 @@
             pltpu.VMEM((6, 16, 768), F32),
             pltpu.VMEM((5, 16, 768), F32),
             pltpu.VMEM((6, 8, 768), F32),
-            dma((N_AG, 9)),
-            dma((N_AG, 9)),
+            dma((N_AG, 13)),
+            dma((N_AG, 13)),
             dma((9, 4)),
             dma((9, 4)),
             dma((9, 6)),
             dma((9, 6)),
             dma((9, 4)),
             dma((9, 4)),
-            dma((13,)),
-            dma((13,)),
+            dma((21,)),
+            dma((21,)),
             dma((35,)),
         ],
         compiler_params=pltpu.CompilerParams(

time: 205 us -> 198 us (0.966)
  Pallas kernels: 202 us -> 195 us
    pallas_call x1, Pallas kernels: 197 us -> 190 us  [fused_step(): pl.pallas_call(fused_kernel, out_shape=(jax.ShapeDtypeStruct((8, 96, widt...]
where the time goes in v4:
time: 198 us
  Pallas kernels  195 us (98%)
  between operations  2.15 us (1%)
    pallas_call x1, Pallas kernels, fused_step(): pl.pallas_call(fused_kernel, out_shape=(jax.ShapeDtypeStruct((8, 96, widt...  190 us
    pallas_call x1, Pallas kernels, fused_step(): pl.pallas_call(finish_kernel, out_shape=(jax.ShapeDtypeStruct((96, 2304),...  5.1 us

profile of v4, /device:TPU:0, one launch (start us, length us, event | category | flops | bytes accessed | tf_op | source)
XLA Modules:
  0.0 197.5 jit_solution(1961979921102325968)
XLA Ops:
  1.9 190.3 %lit_step.1 = (bf16[8,96,768]{2,1,0:T(8,128)(2,1)}, bf16[384,768]{1,0:T(8,128)(2,1)}, bf16[1024,768]{1,0:T(8,128)(2,1)}, f32[16,768]{1,0:T(8,128)}, f32[1,64]{1,0:T(1,128)}) custom-call(f32[1]{0:T(128)S(6)} %copy.29.sharp_ref, f32[1]{0:T(128)S(6)} %copy.30.offset_ref, bf16[1024,768]{1,0:T(8,128)(2,1)} %bitcast.10, s32[16,64]{1,0:T(8,128)} %segment_ref.1, ...), custom_call_target="tpu_custom_call" | custom-call | tf_op jit(solution)/shard_map/lit_step/pallas_call | solution.py:1534
  192.2 5.1 %lit_finish.1 = (f32[96,2304]{1,0:T(8,128)}, f32[96,768]{1,0:T(8,128)}, f32[96,3072]{1,0:T(8,128)}, f32[384,768]{1,0:T(8,128)}, f32[2,96]{1,0:T(2,128)}, /*index...) custom-call(bf16[8,96,768]{2,1,0:T(8,128)(2,1)} %get-tuple-element.23.units_hbm, ...), custom_call_target="tpu_custom_call" | custom-call | tf_op jit(solution)/shard_map/lit_finish/pallas_call | solution.py:1617

commit v5 on v4

--- a/solution.py
+++ b/solution.py
@@ -326,24 +326,22 @@
 ROWS = 128
 GROUPS = 2
 N_AG = 11
-Z_PAIRS = ((0, 1), (3, 4), (6, 7), (9, 10))
+Z_PAIRS = ((0, 1), (3, 4), (6, 7))
 GATHER = {
-    "start": ("o0", "o1", "o7", "o3",),
-    "keys": ("r0", "r1", "o2",),
-    "mixed": ("l0", "r3", "o4",),
-    "image": ("l1", "o6", "r7", "z0", "r2", "l3", "o5",),
-    "norm": ("y0", "r4", "l2",),
-    "project1": ("o10", "r5", "r6",),
-    "project2": ("o9", "l4",),
-    "attend2": ("o8",),
-    "attend4": ("l6", "l7", "z1",),
-    "attend6": ("y1",),
-    "attend7": ("l5",),
-    "out": ("r9", "r10", "z2",),
-    "norm2": ("r8", "y2",),
-    "widen1": ("l8", "l10", "l9",),
-    "widen2": ("z3",),
-    "widen3": ("y3",),
+    "start": ("o1", "o0", "o2",),
+    "mixed": ("r0", "o4", "o6", "r1", "o3",),
+    "image": ("r2", "l1", "l0", "r4", "o7",),
+    "norm": ("z0", "l4", "r3", "o5", "y0", "l2",),
+    "project0": ("r7", "o8",),
+    "project1": ("l3", "r6",),
+    "attend2": ("o9", "r5",),
+    "attend3": ("z1", "y1",),
+    "attend7": ("o10", "l6", "r8", "l7",),
+    "norm2": ("l5", "r9", "z2",),
+    "widen0": ("y2",),
+    "widen1": ("r10",),
+    "widen2": ("l8",),
+    "widen3": ("l10", "l9",),
 }
 D_UNIT = 8
 
@@ -993,11 +991,11 @@
         copy.wait()
 
     def first_norm(i):
-        r = span(32 * i, 32)
+        r = span(ROWS * i, ROWS)
         scaled, _ = norm_rows(h2[r, :].astype(F32))
         h1[r, :] = (scaled * params[0:1, :] + params[6:7, :]).astype(BF)
 
-    loop(32, first_norm)
+    loop(1024 // ROWS, first_norm)
     for group in range(8):
         rows = [segment_ref[2 * group + k : 2 * group + k + 1, :] + CAPS * (2 * group + k) for k in range(2)]
         same = lax.broadcasted_iota(jnp.int32, (64, 128), 0) == jnp.concatenate(rows, axis=1)
@@ -1073,11 +1071,11 @@
     hook("out")
 
     def second_norm(i):
-        r = span(32 * i, 32)
+        r = span(ROWS * i, ROWS)
         scaled, _ = norm_rows(x1[r, :])
         h2[r, :] = (scaled * params[1:2, :] + params[7:8, :]).astype(BF)
 
-    loop(32, second_norm)
+    loop(1024 // ROWS, second_norm)
     hook("norm2")
     face_wait(3)
     face_start(4)
@@ -1086,18 +1084,13 @@
     def widen(j):
         def body(i):
             r = span(TILE * i, TILE)
-            work[...] = nn(h2[r, :], wts[4 + j]) + params[8 + j : 9 + j, :]
-
-            def gelu(k):
-                inner = span(16 * k, 16)
-                hidden = work[inner, :]
+            for at in range(0, 768, 256):
+                hidden = nn(h2[r, :], wts[4 + j, :, pl.ds(at, 256)]) + params[8 + j : 9 + j, at : at + 256]
                 cdf = normal_cdf(hidden)
-                outer = span(TILE * i + 16 * k, 16)
-                act[outer, pl.ds(768 * j, 768)] = (hidden * cdf).astype(BF)
+                cols = pl.ds(768 * j + at, 256)
+                act[r, cols] = (hidden * cdf).astype(BF)
                 slope = cdf + hidden * (jnp.exp(-0.5 * hidden * hidden) * (1.0 / math.sqrt(2.0 * math.pi)))
-                dg[outer, pl.ds(768 * j, 768)] = slope.astype(BF)
-
-            loop(16, gelu)
+                dg[r, cols] = slope.astype(BF)
 
         loop(4, body)
 
@@ -1469,9 +1462,9 @@
         copy.start()
         return copy
 
+    tokens_in = move(input_hbm, tokens, 2)
     units_in = move(units_hbm, units, 0)
     down_in = move(down_hbm, down, 1)
-    tokens_in = move(input_hbm, tokens, 2)
     for shard in range(8):
 
         @pl.when(fs == shard)
@@ -1483,12 +1476,14 @@
                 hidden_out[q : q + 1, :] = small_ref[8 + shard // 2 : 9 + shard // 2, at : at + 128]
 
     loss_out[...] = loss_ref[...]
+    tokens_in.wait()
+    moves = [move(tokens, input_out, 7)]
     units_in.wait()
     for quad in range(3):
         for j in range(3):
             at = 768 * j + 256 * quad
             qkv[:, at : at + 256] = units[quad, :, 256 * j : 256 * j + 256].astype(F32)
-    moves = [move(qkv, qkv_out, 3)]
+    moves.append(move(qkv, qkv_out, 3))
     out[...] = units[3].astype(F32)
     moves.append(move(out, out_out, 4))
     for j in range(4):
@@ -1497,8 +1492,6 @@
     down_in.wait()
     down_wide[...] = down[...].astype(F32)
     moves.append(move(down_wide, down_out, 6))
-    tokens_in.wait()
-    moves.append(move(tokens, input_out, 7))
     for copy in moves:
         copy.wait()
 

time: 198 us -> 186 us (0.939)
  Pallas kernels: 195 us -> 183 us
    pallas_call x1, Pallas kernels: 190 us -> 178 us  [fused_step(): pl.pallas_call(fused_kernel, out_shape=(jax.ShapeDtypeStruct((8, 96, widt...]
where the time goes in v5:
time: 186 us; the launch traced here: 185 us
  Pallas kernels  183 us (98%)
  between operations  2.15 us (1%)
    pallas_call x1, Pallas kernels, fused_step(): pl.pallas_call(fused_kernel, out_shape=(jax.ShapeDtypeStruct((8, 96, widt...  178 us
    pallas_call x1, Pallas kernels, fused_step(): pl.pallas_call(finish_kernel, out_shape=(jax.ShapeDtypeStruct((96, 2304),...  5.18 us

profile of v5, /device:TPU:0, one launch (start us, length us, event | category | flops | bytes accessed | tf_op | source)
XLA Modules:
  0.0 185.4 jit_solution(11397489868715605655)
XLA Ops:
  1.9 178.0 %lit_step.1 = (bf16[8,96,768]{2,1,0:T(8,128)(2,1)}, bf16[384,768]{1,0:T(8,128)(2,1)}, bf16[1024,768]{1,0:T(8,128)(2,1)}, f32[16,768]{1,0:T(8,128)}, f32[1,64]{1,0:T(1,128)}) custom-call(f32[1]{0:T(128)S(6)} %copy.29.sharp_ref, f32[1]{0:T(128)S(6)} %copy.30.offset_ref, bf16[1024,768]{1,0:T(8,128)(2,1)} %bitcast.10, s32[16,64]{1,0:T(8,128)} %segment_ref.1, ...), custom_call_target="tpu_custom_call" | custom-call | tf_op jit(solution)/shard_map/lit_step/pallas_call | solution.py:1527
  180.0 5.2 %lit_finish.1 = (f32[96,2304]{1,0:T(8,128)}, f32[96,768]{1,0:T(8,128)}, f32[96,3072]{1,0:T(8,128)}, f32[384,768]{1,0:T(8,128)}, f32[2,96]{1,0:T(2,128)}, /*index...) custom-call(bf16[8,96,768]{2,1,0:T(8,128)(2,1)} %get-tuple-element.23.units_hbm, ...), custom_call_target="tpu_custom_call" | custom-call | tf_op jit(solution)/shard_map/lit_finish/pallas_call | solution.py:1610
